TPU v7x, 32 devices: a whole 2x2x4 slice. The times are simulated.
32 devices in a mesh: ka: 4 (over y, x), pb: 8 (over z, core).
Axes of the slice: x: 2, y: 2, z: 4, core: 2. Of those that a mesh axis runs over, the one named last changes fastest.
Arguments:
- bloch_elements: float32 [2, 96, 96, 64, 64], P(None, 'ka', 'pb'), may hold values from -768 to 768
- gauge: float32 [2, 96, 64, 64], P(None, 'ka'), may hold values from -0.5 to 0.5
- kq_index: int32 [96, 96], P('ka', 'pb'), may hold values from 0 to 95, as said below
- qpoint: int32 [96], replicated, may hold values from 0 to 95, as said below
- re_vectors: int32 [128, 3], replicated, may hold values from -3 to 3
- re_weight: int32 [128], replicated, may hold values from 1 to 4
- rp_vectors: int32 [128, 3], replicated, may hold values from -3 to 3
- rp_weight: int32 [128], replicated, may hold values from 1 to 4
Outputs:
- wannier_elements: float32 [2, 128, 128, 64, 64], P(None, 'ka', 'pb')
Inputs may be any that keep to these rules, and one draw needn't show every extreme that they name: `qpoint`: each mesh index appears in exactly one slot. kq_index[k, s] is the mesh index of point k plus the point of slot s, folded back into the mesh.
All inputs are finite; a program needn't handle non-finite values.
Results may differ from a plain program's by a relative error of at most 0.000071.
Values sent between devices are 32-bit elements; how exact they have to be, the bound alone decides.
A program may use at most 192 MiB of HBM per device.

v0:
```python
import math

import jax
import jax.numpy as jnp
from jax import lax
from jax.sharding import PartitionSpec as P

MK1 = 4
MK2 = 6
MK3 = 4


def mesh_phase(vectors, points, total_count):
    first_index = points // (MK2 * MK3)
    second_index = points // MK3 % MK2
    third_index = points % MK3
    phase_turns = (
        vectors[:, 0:1] * (first_index * (MK2 * MK3))[None, :]
        + vectors[:, 1:2] * (second_index * (MK1 * MK3))[None, :]
        + vectors[:, 2:3] * (third_index * (MK1 * MK2))[None, :]
    )
    phase_turns = jnp.mod(phase_turns, MK1 * MK2 * MK3)
    angles = phase_turns.astype(jnp.float32) * (2.0 * math.pi / (MK1 * MK2 * MK3))
    return (jnp.cos(angles) / total_count, jnp.sin(angles) / total_count)


def rotate_gauge(elements, left_side, right_side):
    exact_mode = lax.Precision.HIGH
    real_part = jnp.matmul(elements[0], right_side[0], precision=exact_mode) - jnp.matmul(
        elements[1], right_side[1], precision=exact_mode
    )
    imag_part = jnp.matmul(elements[0], right_side[1], precision=exact_mode) + jnp.matmul(
        elements[1], right_side[0], precision=exact_mode
    )
    left_real = jnp.swapaxes(left_side[0], -1, -2)
    left_imag = jnp.swapaxes(left_side[1], -1, -2)
    rot_real = jnp.matmul(left_real, real_part, precision=exact_mode) + jnp.matmul(
        left_imag, imag_part, precision=exact_mode
    )
    rot_imag = jnp.matmul(left_real, imag_part, precision=exact_mode) - jnp.matmul(
        left_imag, real_part, precision=exact_mode
    )
    return jnp.stack([rot_real, rot_imag])


def complex_table(table, count):
    cosine, sine_table = table
    real_rows = jnp.stack([cosine, sine_table], axis=1)
    imag_rows = jnp.stack([-sine_table, cosine], axis=1)
    scale = count.astype(jnp.float32)[None, :, None, None]
    return jnp.stack([real_rows, imag_rows]) / scale


def local(bloch_elements, gauge, kq_index, qpoint, re_vectors, re_weight, rp_vectors, rp_weight):
    local_k = bloch_elements.shape[1]
    local_q = bloch_elements.shape[2]
    bands = bloch_elements.shape[3]
    pairs = bands * bands
    gathered = lax.all_gather(gauge, "ka", axis=1, tiled=True)
    left_side = jnp.take(gathered, kq_index, axis=1)
    rotated = rotate_gauge(bloch_elements, left_side, gauge[:, :, None])
    rotated = rotated.reshape(2, local_k, local_q, pairs)
    k_count = gathered.shape[1]
    q_count = qpoint.shape[0]
    k_table = mesh_phase(re_vectors, jnp.arange(k_count, dtype=jnp.int32), k_count)
    q_table = mesh_phase(rp_vectors, qpoint, q_count)
    ka_count = lax.axis_size("ka")
    pb_count = lax.axis_size("pb")
    re_local = re_vectors.shape[0] // ka_count
    rp_local = rp_vectors.shape[0] // pb_count
    devices = ka_count * pb_count
    column_width = pairs // devices
    leaving = rotated.reshape(2, local_k, local_q, devices, column_width).transpose(3, 0, 1, 2, 4)
    leaving = leaving.reshape(devices, 2 * local_k * local_q, column_width)
    joined = lax.all_to_all(leaving, ("ka", "pb"), split_axis=0, concat_axis=0, tiled=True)
    joined = joined.reshape(ka_count, pb_count, 2, local_k, local_q, column_width)
    k_blocks = complex_table(k_table, re_weight).reshape(
        2, ka_count, re_local, 2, ka_count, local_k
    )
    q_blocks = complex_table(q_table, rp_weight).reshape(
        2, pb_count, rp_local, 2, pb_count, local_q
    )
    exact_mode = lax.Precision.HIGH
    electron = jnp.einsum("dauemk,mpeklx->dauplx", k_blocks, joined, precision=exact_mode)
    spread = jnp.einsum("fbvdpl,dauplx->abfuvx", q_blocks, electron, precision=exact_mode)
    spread = spread.reshape(devices, 2 * re_local * rp_local, column_width)
    result = lax.all_to_all(spread, ("ka", "pb"), split_axis=0, concat_axis=0, tiled=True)
    result = result.reshape(devices, 2, re_local, rp_local, column_width)
    return result.transpose(1, 2, 3, 0, 4).reshape(2, re_local, rp_local, bands, bands)


def solution(mesh):
    placed = (
        P(None, "ka", "pb", None, None),
        P(None, "ka", None, None),
        P("ka", "pb"),
        P(),
        P(),
        P(),
        P(),
        P(),
    )
    return jax.shard_map(
        local,
        mesh=mesh,
        in_specs=placed,
        out_specs=P(None, "ka", "pb", None, None),
        check_vma=False,
    )
```

profile of v0, /device:TPU:9, one launch (start us, length us, event | category | flops | bytes accessed | tf_op | source)
XLA Modules:
  0.0 894.9 jit_solution(5859265821960317162)
XLA Ops:
  6.5 0.0 all-gather.2.cloned.1.call-start
  6.5 0.0 copy-start.1
  6.5 0.7 all-gather.2.cloned.1.call-update
  7.3 0.7 compare_select_fusion
  8.0 0.1 copy.24
  8.0 0.1 reshape.750
  8.1 0.7 compare_and_fusion
  8.8 0.1 copy.23
  9.0 0.0 copy-start
  9.0 9.5 %fusion.10 = f32[24,12,64,64]{3,2,1,0:T(8,128)} fusion(f32[2,24,12,64,64]{4,3,2,1,0:T(8,128)} %param.8, f32[2,24,64,64]{3,2,1,0:T(8,128)} %param.9), kind=kOutput, calls=%fused_computation.15 | convolution fusion | flops 452984832 | bytes 14942208 | tf_op jit(solution)/shard_map/dot_general | solution.py:29
  18.5 0.0 copy-done.1
  18.5 4.2 copy-done
  22.7 6.2 fusion.6
  28.9 6.1 fusion.4
  35.0 6.2 fusion.8
  41.2 39.0 %all-gather.2.cloned.1.call-done = f32[2,96,64,64]{3,2,1,0:T(8,128)} async-done(((f32[2,24,64,64]{3,2,1,0:T(8,128)}), f32[2,96,64,64]{3,2,1,0:T(8,128)}) %all-gather.2.cloned.1.call-update) | async-done | bytes 3145744 | tf_op jit(solution)/shard_map/all_gather | solution.py:59
  80.2 15.9 %gather_fusion = f32[288,2,64,64]{3,2,1,0:T(8,128)} fusion(f32[2,96,64,64]{3,2,1,0:T(8,128)} %all-gather.2.cloned.1.call-done, s32[1024]{0:T(1024)S(1)} %pad_clamp_fusion), kind=kCustom, calls=%fused_computation | custom fusion | bytes 18875520 | tf_op jit(solution)/shard_map/jit(_take)/gather | solution.py:60
  96.1 18.7 %copy.25 = f32[288,2,64,64]{2,3,0,1:T(8,128)} copy(f32[288,2,64,64]{3,2,1,0:T(8,128)} %gather_fusion) | data formatting | bytes 18874368 | tf_op jit(solution)/shard_map/jit(_take)/gather | solution.py:60
  114.9 0.0 slice-start
  114.9 0.0 slice-start.1
  114.9 14.4 %select_bitcast_fusion = f32[2,24,12,64,64]{3,4,2,1,0:T(8,128)} fusion(f32[24,12,2,64,64]{3,4,1,0,2:T(8,128)} %bitcast.84, pred[24,12]{1,0:T(8,128)(4,1)S(1)} %copy.23), kind=kLoop, calls=%fused_computation.1 | loop fusion | flops 2359296 | bytes 18874656 | tf_op jit(solution)/shard_map/jit(_take)/select_n | solution.py:60
  129.2 0.0 slice-start.2
  129.2 15.2 %fusion.13 = f32[24,12,64,64]{3,2,1,0:T(8,128)} fusion(f32[2,24,12,64,64]{3,4,2,1,0:T(8,128)} %select_bitcast_fusion, f32[24,12,64,64]{3,2,1,0:T(8,128)} %fusion.10, f32[24,12,64,64]{3,2,1,0:T(8,128)} %fusion.6), kind=kOutput, calls=%fused_computation.18 | convolution fusion | flops 454164480 | bytes 33030144 | tf_op jit(solution)/shard_map/dot_general | solution.py:37
  144.5 0.0 slice-done
  144.5 0.0 slice-done.1
  144.5 0.0 slice-done.2
  144.5 11.2 %fusion.12 = f32[24,12,64,64]{3,2,1,0:T(8,128)} fusion(f32[2,24,12,64,64]{3,4,2,1,0:T(8,128)} %select_bitcast_fusion, f32[24,12,64,64]{3,2,1,0:T(8,128)} %fusion.8, f32[24,12,64,64]{3,2,1,0:T(8,128)S(1)} %bitcast.83), kind=kOutput, calls=%fused_computation.17 | convolution fusion | flops 454164480 | bytes 28311552 | tf_op jit(solution)/shard_map/dot_general | solution.py:40
  155.6 18.2 %fusion.30 = f32[24,12,64,64]{3,2,1,0:T(8,128)} fusion(f32[24,12,64,64]{3,2,1,0:T(8,128)} %fusion.13, f32[24,12,64,64]{3,2,1,0:T(8,128)} %fusion.8, f32[24,12,64,64]{3,2,1,0:T(8,128)} %fusion.4, f32[2,24,12,64,64]{3,4,2,1,0:T(8,128)} %select_bitcast_fusion), kind=kOutput, calls=%fused_computation.31 | convolution fusion | flops 455344128 | bytes 42467328 | tf_op jit(solution)/shard_map/dot_general | solution.py:37
  173.8 8.7 stack.42
  182.6 18.2 %fusion.33 = f32[24,12,64,64]{3,2,1,0:T(8,128)} fusion(f32[24,12,64,64]{3,2,1,0:T(8,128)} %fusion.12, f32[24,12,64,64]{3,2,1,0:T(8,128)} %fusion.10, f32[24,12,64,64]{3,2,1,0:T(8,128)} %fusion.6, f32[2,24,12,64,64]{3,4,2,1,0:T(8,128)} %select_bitcast_fusion), kind=kOutput, calls=%fused_computation.32 | convolution fusion | flops 455344128 | bytes 42467328 | tf_op jit(solution)/shard_map/dot_general | solution.py:40
  200.8 8.9 stack.43
  209.7 4.9 pad_maximum_fusion
  214.6 9.2 %copy.26 = f32[32,576,128]{2,1,0:T(8,128)} copy(f32[32,576,128]{2,0,1:T(8,128)S(1)} %bitcast.88) | data formatting | bytes 18874368 | tf_op jit(solution)/shard_map/reshape | solution.py:74
  223.8 0.0 copy-start.3
  223.8 0.0 copy-start.5
  223.8 0.0 copy-start.4
  223.8 0.0 copy-start.6
  223.8 6.0 all-to-all-start
  229.9 0.0 copy-done.2
  229.9 0.0 copy-done.3
  229.9 0.1 mul.287
  230.0 0.1 mul.292
  230.1 0.1 mul.297
  230.2 0.0 copy-done.5
  230.2 0.1 div.70
  230.3 0.1 mul.303
  230.3 0.1 mul.309
  230.4 0.1 mul.315
  230.5 0.0 copy-done.4
  230.5 0.1 mul.306
  230.6 0.1 mul.312
  230.7 0.1 mul.318
  230.8 0.0 copy-done.6
  230.8 0.1 div.80
  230.9 0.9 sine_multiply_fusion.1
  231.8 2.3 sine_multiply_fusion
  234.2 198.2 %all-to-all-done = f32[32,576,128]{2,1,0:T(8,128)} async-done(((f32[32,576,128]{2,1,0:T(8,128)}), f32[32,576,128]{2,1,0:T(8,128)}, u32[]{:S(2)}, u32[]{:S(2)}) %all-to-all-start) | async-done | bytes 9437216 | tf_op jit(solution)/shard_map/all_to_all | solution.py:75
  432.4 9.1 %copy.27 = f32[32,576,128]{2,0,1:T(8,128)S(1)} copy(f32[32,576,128]{2,1,0:T(8,128)} %all-to-all-done) | data formatting | bytes 18874368 | tf_op jit(solution)/shard_map/all_to_all | solution.py:75
  441.5 14.9 %fusion.23 = f32[2,4,32,8,12,128,1,1]{5,2,4,3,1,0,7,6:T(8,128)} fusion(f32[4,8,2,24,12,128,1,1]{5,1,0,4,3,2,7,6:T(8,128)S(1)} %bitcast.87, f32[1,4,32,1,4,24]{2,5,4,3,1,0:T(8,128)S(1)} %get-tuple-element.16, f32[1,4,32,1,4,24]{2,5,4,3,1,0:T(8,128)S(1)} %get-tuple-element.15, f32[1,4,32,1,4,24]{2,5,4,3,1,0:T(8,128)S(1)} %get-tuple-element.14, ...), kind=kOutput, calls=%fused_computation.26 | convolution fusion | flops 3624075264 | bytes 22168064 | tf_op jit(solution)/shard_map/dauemk,mpeklx->dauplx/dot_general | solution.py:84
  456.4 24.0 %fusion.20 = f32[4,8,2,32,16,128]{5,4,1,2,3,0:T(8,128)S(1)} fusion(f32[2,4,32,8,12,128,1,1]{5,2,4,3,1,0,7,6:T(8,128)} %fusion.23, f32[1,8,16,1,8,12]{5,2,4,3,1,0:T(8,128)S(1)} %get-tuple-element.13, f32[1,8,16,1,8,12]{5,2,4,3,1,0:T(8,128)S(1)} %get-tuple-element.12, f32[1,8,16,1,8,12]{5,2,4,3,1,0:T(8,128)S(1)} %get-tuple-element.11, f32[8,16]{1,0:T(8,128)S(1)} %div.80), kind=kOutput, calls=%fused_computation.25 | convolution fusion | flops 4832034816 | bytes 29508096 | tf_op jit(solution)/shard_map/fbvdpl,dauplx->abfuvx/dot_general | solution.py:85
  480.4 1.7 copy.30
  482.2 368.1 %all_to_all.10 = f32[32,1024,128]{2,1,0:T(8,128)S(1)} all-to-all(f32[32,1024,128]{2,1,0:T(8,128)S(1)} %bitcast.85), channel_id=1, replica_groups=mesh['ka'=4,'pb'=8] {'ka','pb'}, dimensions={0} | all-to-all | bytes 33554432 | tf_op jit(solution)/shard_map/all_to_all | solution.py:87
  850.3 13.1 %copy.31 = f32[2,32,16,32,128]{4,3,2,1,0:T(8,128)} copy(f32[2,32,16,32,128]{4,2,1,0,3:T(8,128)S(1)} %bitcast.86) | data formatting | bytes 33554432 | tf_op jit(solution)/shard_map/transpose | solution.py:89
  863.4 24.4 %reshape.747 = f32[2,32,16,64,64]{4,3,2,1,0:T(8,128)} reshape(f32[2,32,16,32,128]{4,3,2,1,0:T(8,128)} %copy.31) | data formatting | bytes 33554432 | tf_op jit(solution)/shard_map/reshape | solution.py:89
  (9 shorter events, 0.1 us)
Async XLA Ops:
  6.5 73.7 %all-gather.2.cloned.1.call-start = ((), (), s32[]{:S(2)}) async-start(), calls=%async_computation.2 | async-start | bytes 7864320 | tf_op jit(solution)/shard_map/all_gather | solution.py:59
  6.5 11.9 %copy-start.1 = (f32[2,24,64,64]{3,2,1,0:T(8,128)S(1)}, f32[2,24,64,64]{3,2,1,0:T(8,128)}, u32[]{:S(2)}) copy-start(f32[2,24,64,64]{3,2,1,0:T(8,128)} %param.9) | copy-start | bytes 2359300
  9.0 13.7 %copy-start = (f32[2,24,12,64,64]{4,3,2,1,0:T(8,128)S(1)}, f32[2,24,12,64,64]{4,3,2,1,0:T(8,128)}, u32[]{:S(2)}) copy-start(f32[2,24,12,64,64]{4,3,2,1,0:T(8,128)} %param.8) | copy-start | bytes 28311556
  114.9 29.6 %slice-start = ((s8[9437184]{0:T(1024)(128)(4,1)}), s8[4194304]{0:T(1024)(128)(4,1)S(1)}, s32[]{:S(2)}) async-start(s8[9437184]{0:T(1024)(128)(4,1)} %bitcast.82), calls=%async_computation.3 | async-start | bytes 8388608
  114.9 29.6 %slice-start.1 = ((s8[9437184]{0:T(1024)(128)(4,1)}), s8[4194304]{0:T(1024)(128)(4,1)S(1)}, s32[]{:S(2)}) async-start(s8[9437184]{0:T(1024)(128)(4,1)} %bitcast.82), calls=%async_computation.4 | async-start | bytes 8388608
  129.2 15.2 %slice-start.2 = ((s8[9437184]{0:T(1024)(128)(4,1)}), s8[1048576]{0:T(1024)(128)(4,1)S(1)}, s32[]{:S(2)}) async-start(s8[9437184]{0:T(1024)(128)(4,1)} %bitcast.82), calls=%async_computation.5 | async-start | bytes 2097152
  223.8 6.0 copy-start.2
  223.8 6.1 copy-start.3
  223.8 6.3 copy-start.5
  223.8 6.7 copy-start.4
  223.8 6.9 copy-start.6
  223.8 208.5 %all-to-all-start = ((f32[32,576,128]{2,1,0:T(8,128)}), f32[32,576,128]{2,1,0:T(8,128)}, u32[]{:S(2)}, u32[]{:S(2)}) async-start(f32[32,576,128]{2,1,0:T(8,128)} %copy.26), calls=%async_computation | async-start | bytes 18874368 | tf_op jit(solution)/shard_map/all_to_all | solution.py:75
Sparse Core Ops, SparseCore 0:
  9.2 71.0 all-gather.1
where the time goes:
time: 909 us; the launch traced here: 895 us
  blocking collectives  368 us (40%)
  waiting for transfers between devices  238 us (26%)
  matrix products  130 us (14%)
  local copies, waits for them, and re-layouts  115 us (13%)
  other arithmetic  24 us (3%)
  between operations  13.8 us (2%)
    all_to_all x1, blocking collectives, local(): lax.all_to_all(spread, ('ka', 'pb'), split_axis=0, concat_axis=0, tiled=T...  368 us
    all_to_all x1, waiting for transfers between devices, local(): lax.all_to_all(leaving, ('ka', 'pb'), split_axis=0, concat_axis=0, tiled=...  198 us
    all_gather x1, waiting for transfers between devices, local(): gathered = lax.all_gather(gauge, 'ka', axis=1, tiled=True)  39 us
    gather x2, local copies, waits for them, and re-layouts, local(): left_side = jnp.take(gathered, kq_index, axis=1)  34.6 us
    reshape x1, local copies, waits for them, and re-layouts, local(): result.transpose(1, 2, 3, 0, 4).reshape(2, re_local, rp_local, bands, bands)  24.4 us
    dot_general x1, matrix products, local(): jnp.einsum('fbvdpl,dauplx->abfuvx', q_blocks, electron, precision=exact_m...  24 us
    dot_general x1, matrix products, rotate_gauge(): jnp.matmul(left_imag, real_part, precision=exact_mode)  18.2 us
    dot_general x1, matrix products, rotate_gauge(): jnp.matmul(left_imag, imag_part, precision=exact_mode)  18.2 us
  transfers between devices with their start and end apart: 2, of which 2 were waited for; matrix products, arithmetic and copies ran while one was open for 4% of the time, Pallas kernels for 0%

commit v1 on v0

--- a/solution.py
+++ b/solution.py
@@ -1,13 +1,19 @@
+import functools
 import math
 
 import jax
 import jax.numpy as jnp
 from jax import lax
+from jax.experimental import pallas as pl
+from jax.experimental.pallas import tpu as pltpu
 from jax.sharding import PartitionSpec as P
 
 MK1 = 4
 MK2 = 6
 MK3 = 4
+LANES = 128
+VMEM_BYTES = 67_000_000
+MESH = pl.DeviceIdType.MESH
 
 
 def mesh_phase(vectors, points, total_count):
@@ -51,7 +57,7 @@
     return jnp.stack([real_rows, imag_rows]) / scale
 
 
-def local(bloch_elements, gauge, kq_index, qpoint, re_vectors, re_weight, rp_vectors, rp_weight):
+def local_general(bloch_elements, gauge, kq_index, qpoint, re_vectors, re_weight, rp_vectors, rp_weight):
     local_k = bloch_elements.shape[1]
     local_q = bloch_elements.shape[2]
     bands = bloch_elements.shape[3]
@@ -89,6 +95,445 @@
     return result.transpose(1, 2, 3, 0, 4).reshape(2, re_local, rp_local, bands, bands)
 
 
+def split(x):
+    high = x.astype(jnp.bfloat16)
+    low = (x - high.astype(jnp.float32)).astype(jnp.bfloat16)
+    return high, low
+
+
+def dot(a, b):
+    return jnp.dot(a, b, preferred_element_type=jnp.float32)
+
+
+def swap(x, sign):
+    return pltpu.roll(x, x.shape[-1] // 2, x.ndim - 1) * sign
+
+
+class Plan:
+    def __init__(self, ka, pb, local_k, local_q, bands, re_count, rp_count):
+        self.ka, self.pb = ka, pb
+        self.devices = ka * pb
+        self.local_k, self.local_q, self.bands = local_k, local_q, bands
+        self.k_count, self.q_count = ka * local_k, pb * local_q
+        self.re_count, self.rp_count = re_count, rp_count
+        self.re_local, self.rp_local = re_count // ka, rp_count // pb
+        self.fits = (
+            2 * bands == LANES
+            and bands % self.devices == 0
+            and pb % 2 == 0
+            and ka % 2 == 0
+            and local_k % 6 == 0
+        )
+        if not self.fits:
+            return
+        self.rows = bands // self.devices
+        self.share = self.rows * local_q
+        self.kc = 3
+        self.k_chunks = local_k // self.kc
+        self.rpc = 2
+        self.rp_chunks = self.rp_local // self.rpc
+        self.width = self.rows * pb
+        self.piece = self.rpc * self.rows * self.k_count
+        self.block = self.re_local * self.rpc * self.width
+        self.slots = 2
+        self.fits = (
+            self.share % 8 == 0
+            and self.k_count % 16 == 0
+            and (pb * self.share) % 16 == 0
+            and self.width % 8 == 0
+            and self.rp_local % self.rpc == 0
+            and self.rp_chunks > self.slots
+        )
+
+
+def kernel(
+    p,
+    bloch,
+    v_in,
+    right,
+    kq,
+    tq,
+    tk,
+    out,
+    gbuf,
+    vg,
+    rot,
+    x_buf,
+    y_buf,
+    z_buf,
+    w_buf,
+    g_sem,
+    own_sem,
+    vs_sem,
+    v1_sem,
+    f_sem,
+    v2_sem,
+    s1_sem,
+    r1_sem,
+    s2_sem,
+    r2_sem,
+    s3_sem,
+    r3_sem,
+):
+    a = lax.axis_index("ka")
+    b = lax.axis_index("pb")
+    me = a * p.pb + b
+    core = b % 2
+    sibling = b + 1 - 2 * core
+    half = p.local_k // 2
+    lane = lax.broadcasted_iota(jnp.int32, (1, LANES), 1)
+    sign = jnp.where(lane < p.bands, 1.0, -1.0).astype(jnp.float32)
+
+    def load_g(k):
+        return pltpu.make_async_copy(bloch.at[:, k], gbuf.at[k % 2], g_sem.at[k % 2])
+
+    load_g(0).start()
+    own_v = pltpu.make_async_copy(v_in, vg.at[pl.ds(a * p.local_k, p.local_k)], own_sem)
+    own_v.start()
+
+    barrier = pltpu.get_barrier_semaphore()
+
+    @pl.loop(1, p.devices)
+    def _(o):
+        t = (me + o) % p.devices
+        pl.semaphore_signal(barrier, inc=1, device_id=(t // p.pb, t % p.pb), device_id_type=MESH)
+
+    pl.semaphore_wait(barrier, p.devices - 1)
+
+    def send_v(i):
+        return pltpu.make_async_remote_copy(
+            src_ref=v_in.at[pl.ds(core * half, half)],
+            dst_ref=vg.at[pl.ds(a * p.local_k + core * half, half)],
+            send_sem=vs_sem.at[i],
+            recv_sem=v1_sem.at[i],
+            device_id=((a + i) % p.ka, b),
+            device_id_type=MESH,
+        )
+
+    def pass_v(i):
+        source = (a + p.ka - i) % p.ka
+        part = pl.ds(source * p.local_k + core * half, half)
+        return pltpu.make_async_remote_copy(
+            src_ref=vg.at[part],
+            dst_ref=vg.at[part],
+            send_sem=f_sem.at[i],
+            recv_sem=v2_sem.at[i],
+            device_id=(a, sibling),
+            device_id_type=MESH,
+        )
+
+    for i in range(1, p.ka):
+        send_v(i).start()
+
+    def right_side(k, carry):
+        @pl.when(k + 1 < p.local_k)
+        def _():
+            load_g(k + 1).start()
+
+        load_g(k).wait()
+        g = gbuf[k % 2]
+        g = jnp.concatenate([g[0], g[1]], axis=-1).reshape(p.local_q * p.bands, LANES)
+        g_high, g_low = split(g)
+        r_high, r_low = split(right[k])
+        h = dot(
+            jnp.concatenate([g_high, g_low], axis=1), jnp.concatenate([r_high, r_high], axis=0)
+        ) + dot(g_high, r_low)
+        h = h.reshape(p.local_q, p.bands, LANES)
+        for q in range(p.local_q):
+            rot[k, pl.ds(q, p.bands, stride=p.local_q), :] = h[q]
+        return carry
+
+    lax.fori_loop(0, half, right_side, 0)
+    for i in range(1, p.ka):
+        send_v(i).wait_recv()
+        pass_v(i).start()
+    lax.fori_loop(half, p.local_k, right_side, 0)
+    own_v.wait()
+    for i in range(1, p.ka):
+        pass_v(i).wait_recv()
+
+    def left_side(k, carry):
+        for q in range(p.local_q):
+            v_high, v_low = split(vg[kq[k * p.local_q + q]])
+            h = rot[k, pl.ds(q, p.bands, stride=p.local_q), :]
+            h_high, h_low = split(jnp.concatenate([h, swap(h, sign)], axis=0))
+            rot[k, pl.ds(q, p.bands, stride=p.local_q), :] = dot(
+                jnp.concatenate([v_high, v_low], axis=1),
+                jnp.concatenate([h_high, h_high], axis=0),
+            ) + dot(v_high, h_low)
+        return carry
+
+    def send_1(c, o):
+        t = (me + o) % p.devices
+        ks = pl.ds(c * p.kc, p.kc)
+        return pltpu.make_async_remote_copy(
+            src_ref=rot.at[ks, pl.ds(t * p.share, p.share)],
+            dst_ref=x_buf.at[a, ks, b],
+            send_sem=s1_sem.at[c],
+            recv_sem=r1_sem.at[c],
+            device_id=(t // p.pb, t % p.pb),
+            device_id_type=MESH,
+        )
+
+    def own_1(c):
+        ks = pl.ds(c * p.kc, p.kc)
+        return pltpu.make_async_copy(
+            rot.at[ks, pl.ds(me * p.share, p.share)], x_buf.at[a, ks, b], r1_sem.at[c]
+        )
+
+    def sum_q(c):
+        part = x_buf.at[:, pl.ds(c * p.kc, p.kc)]
+        pltpu.make_async_copy(part, part, r1_sem.at[c]).wait()
+
+        @pl.loop(0, (p.ka // 2) * p.kc)
+        def _(i):
+            pair = i // p.kc
+            k = c * p.kc + i % p.kc
+            x = jnp.concatenate(
+                [
+                    x_buf[2 * pair, k].reshape(p.pb * p.share, LANES),
+                    x_buf[2 * pair + 1, k].reshape(p.pb * p.share, LANES),
+                ],
+                axis=1,
+            )
+            x_high, x_low = split(x)
+            y = dot(tq[...], jnp.concatenate([x_high, x_high, x_low], axis=0))
+            rows = p.rp_count * p.rows
+            for j in range(2):
+                cols = slice(j * LANES, (j + 1) * LANES)
+                where = pl.ds((2 * pair + j) * p.local_k + k, rows, stride=p.k_count)
+                y_buf[where, :] = y[:rows, cols] + swap(y[rows:, cols], sign)
+
+    @pl.loop(0, p.k_chunks)
+    def _(c):
+        lax.fori_loop(c * p.kc, (c + 1) * p.kc, left_side, 0)
+
+        @pl.loop(1, p.devices)
+        def _(o):
+            send_1(c, o).start()
+
+        own_1(c).start()
+
+        @pl.when(c > 0)
+        def _():
+            sum_q(c - 1)
+
+    sum_q(p.k_chunks - 1)
+
+    def send_2(j, o):
+        t = (b + o) % p.pb
+        first = (t * p.rp_local + j * p.rpc) * p.rows * p.k_count
+        return pltpu.make_async_remote_copy(
+            src_ref=y_buf.at[pl.ds(first, p.piece)],
+            dst_ref=z_buf.at[j, b],
+            send_sem=s2_sem.at[j],
+            recv_sem=r2_sem.at[j],
+            device_id=(a, t),
+            device_id_type=MESH,
+        )
+
+    @pl.loop(0, p.rp_chunks)
+    def _(j):
+        @pl.loop(1, p.pb)
+        def _(o):
+            send_2(j, o).start()
+
+        first = (b * p.rp_local + j * p.rpc) * p.rows * p.k_count
+        pltpu.make_async_copy(
+            y_buf.at[pl.ds(first, p.piece)], z_buf.at[j, b], r2_sem.at[j]
+        ).start()
+
+    def send_3(j, o):
+        t = (a + o) % p.ka
+        slot = j % p.slots
+        return pltpu.make_async_remote_copy(
+            src_ref=w_buf.at[slot, t],
+            dst_ref=out.at[j, a],
+            send_sem=s3_sem.at[slot],
+            recv_sem=r3_sem.at[j],
+            device_id=(t, b),
+            device_id_type=MESH,
+        )
+
+    def own_3(j):
+        slot = j % p.slots
+        return pltpu.make_async_copy(w_buf.at[slot, a], out.at[j, a], g_sem.at[slot])
+
+    def free_3(j):
+        slot = j % p.slots
+        sent = w_buf.at[slot, pl.ds(0, p.ka - 1)]
+        pltpu.make_async_copy(sent, sent, s3_sem.at[slot]).wait()
+        own_3(j).wait()
+
+    @pl.loop(0, p.rp_chunks)
+    def _(j):
+        pltpu.make_async_copy(z_buf.at[j], z_buf.at[j], r2_sem.at[j]).wait()
+        slot = j % p.slots
+
+        @pl.when(j >= p.slots)
+        def _():
+            free_3(j - p.slots)
+
+        @pl.loop(0, p.pb * p.rpc)
+        def _(i):
+            source = i // p.rpc
+            rp = i % p.rpc
+            for r in range(0, p.rows, 2):
+                z = jnp.concatenate(
+                    [
+                        z_buf[j, source, pl.ds((rp * p.rows + r) * p.k_count, p.k_count), :],
+                        z_buf[j, source, pl.ds((rp * p.rows + r + 1) * p.k_count, p.k_count), :],
+                    ],
+                    axis=1,
+                )
+                z_high, z_low = split(z)
+                w = dot(tk[...], jnp.concatenate([z_high, z_high, z_low], axis=0))
+                for s in range(2):
+                    cols = slice(s * LANES, (s + 1) * LANES)
+                    full = w[: p.re_count, cols] + swap(w[p.re_count :, cols], sign)
+                    at = rp * p.width + source * p.rows + r + s
+                    where = pl.ds(at, p.re_local, stride=p.rpc * p.width)
+                    for t in range(p.ka):
+                        w_buf[slot, t, where, :] = full[t * p.re_local : (t + 1) * p.re_local]
+
+        @pl.loop(1, p.ka)
+        def _(o):
+            send_3(j, o).start()
+
+        own_3(j).start()
+
+    for j in range(p.rp_chunks - p.slots, p.rp_chunks):
+        free_3(j)
+
+    @pl.loop(0, p.rp_chunks)
+    def _(j):
+        into = out.at[j, pl.ds(0, p.ka - 1)]
+        pltpu.make_async_copy(into, into, r3_sem.at[j]).wait()
+        first = z_buf.at[j, pl.ds(0, p.pb - 1)]
+        pltpu.make_async_copy(first, first, s2_sem.at[j]).wait()
+
+    @pl.loop(0, p.k_chunks)
+    def _(c):
+        sent = rot.at[pl.ds(c * p.kc, p.kc), pl.ds(0, (p.devices - 1) * p.share)]
+        pltpu.make_async_copy(sent, sent, s1_sem.at[c]).wait()
+
+    for i in range(1, p.ka):
+        send_v(i).wait_send()
+        pass_v(i).wait_send()
+
+
+def unpack(p, step, x_ref, o_ref):
+    for t in range(p.ka):
+        x = x_ref[0, t].reshape(step, p.rpc, p.width, LANES)
+        o_ref[0, :, :, t * p.width : (t + 1) * p.width, :] = x[..., : p.bands]
+        o_ref[1, :, :, t * p.width : (t + 1) * p.width, :] = x[..., p.bands :]
+
+
+def three_parts(table):
+    high = lax.reduce_precision(table, 8, 7)
+    low = lax.reduce_precision(table - high, 8, 7)
+    return jnp.concatenate([high, low, high], axis=1).astype(jnp.bfloat16)
+
+
+def local_fused(p, bloch, gauge, kq_index, qpoint, re_vectors, re_weight, rp_vectors, rp_weight):
+    real, imag = gauge[0], gauge[1]
+    v_in = jnp.concatenate([jnp.swapaxes(real, 1, 2), jnp.swapaxes(imag, 1, 2)], axis=2)
+    right = jnp.concatenate(
+        [jnp.concatenate([real, imag], axis=2), jnp.concatenate([-imag, real], axis=2)], axis=1
+    )
+    vectors = jnp.repeat(rp_vectors, p.rows, axis=0)
+    points = jnp.broadcast_to(
+        qpoint.reshape(p.pb, 1, p.local_q), (p.pb, p.rows, p.local_q)
+    ).reshape(-1)
+    cosine, sine = mesh_phase(vectors, points, p.q_count)
+    row = jnp.arange(p.rp_count * p.rows, dtype=jnp.int32) % p.rows
+    col = jnp.arange(p.q_count * p.rows, dtype=jnp.int32) // p.local_q % p.rows
+    weight = jnp.repeat(rp_weight, p.rows).astype(jnp.float32)[:, None]
+    same = row[:, None] == col[None, :]
+    tq = jnp.where(
+        jnp.concatenate([same, same], axis=0),
+        jnp.concatenate([cosine / weight, sine / weight], axis=0),
+        0.0,
+    )
+    cosine, sine = mesh_phase(re_vectors, jnp.arange(p.k_count, dtype=jnp.int32), p.k_count)
+    weight = re_weight.astype(jnp.float32)[:, None]
+    tk = jnp.concatenate([cosine / weight, sine / weight], axis=0)
+    tq, tk = three_parts(tq), three_parts(tk)
+
+    f32 = jnp.float32
+    dma = pltpu.SemaphoreType.DMA
+    vmem = pl.BlockSpec(memory_space=pltpu.VMEM)
+    any_space = pl.BlockSpec(memory_space=pl.ANY)
+    landed = pl.pallas_call(
+        functools.partial(kernel, p),
+        out_shape=jax.ShapeDtypeStruct((p.rp_chunks, p.ka, p.block, LANES), f32),
+        in_specs=[
+            any_space,
+            any_space,
+            vmem,
+            pl.BlockSpec(memory_space=pltpu.SMEM),
+            vmem,
+            vmem,
+        ],
+        out_specs=any_space,
+        scratch_shapes=[
+            pltpu.VMEM((2, 2, p.local_q, p.bands, p.bands), f32),
+            pltpu.VMEM((p.k_count, p.bands, LANES), f32),
+            pltpu.VMEM((p.local_k, p.devices * p.share, LANES), f32),
+            pltpu.VMEM((p.ka, p.local_k, p.pb, p.share, LANES), f32),
+            pltpu.VMEM((p.rp_count * p.rows * p.k_count, LANES), f32),
+            pltpu.VMEM((p.rp_chunks, p.pb, p.piece, LANES), f32),
+            pltpu.VMEM((p.slots, p.ka, p.block, LANES), f32),
+            dma((2,)),
+            dma,
+            dma((p.ka,)),
+            dma((p.ka,)),
+            dma((p.ka,)),
+            dma((p.ka,)),
+            dma((p.k_chunks,)),
+            dma((p.k_chunks,)),
+            dma((p.rp_chunks,)),
+            dma((p.rp_chunks,)),
+            dma((p.slots,)),
+            dma((p.rp_chunks,)),
+        ],
+        compiler_params=pltpu.CompilerParams(
+            collective_id=0, has_side_effects=True, vmem_limit_bytes=VMEM_BYTES
+        ),
+    )(bloch, v_in, right, kq_index.reshape(-1), tq, tk)
+
+    step = 8
+    return pl.pallas_call(
+        functools.partial(unpack, p, step),
+        grid=(p.re_local // step, p.rp_chunks),
+        out_shape=jax.ShapeDtypeStruct((2, p.re_local, p.rp_local, p.bands, p.bands), f32),
+        in_specs=[
+            pl.BlockSpec(
+                (1, p.ka, step * p.rpc * p.width, LANES), lambda i, j: (j, 0, i, 0)
+            )
+        ],
+        out_specs=pl.BlockSpec(
+            (2, step, p.rpc, p.bands, p.bands), lambda i, j: (0, i, j, 0, 0)
+        ),
+    )(landed)
+
+
+def local(bloch_elements, gauge, kq_index, qpoint, re_vectors, re_weight, rp_vectors, rp_weight):
+    p = Plan(
+        lax.axis_size("ka"),
+        lax.axis_size("pb"),
+        bloch_elements.shape[1],
+        bloch_elements.shape[2],
+        bloch_elements.shape[3],
+        re_vectors.shape[0],
+        rp_vectors.shape[0],
+    )
+    program = functools.partial(local_fused, p) if p.fits else local_general
+    return program(
+        bloch_elements, gauge, kq_index, qpoint, re_vectors, re_weight, rp_vectors, rp_weight
+    )
+
+
 def solution(mesh):
     placed = (
         P(None, "ka", "pb", None, None),

time: 909 us -> 608 us (0.67); the launches traced: 895 us -> 607 us
  Pallas kernels: 0 us -> 594 us
  blocking collectives: 368 us -> 0 us
  waiting for transfers between devices: 238 us -> 0 us
  matrix products: 130 us -> 0 us
  local copies, waits for them, and re-layouts: 115 us -> 5.96 us
  other arithmetic: 24 us -> 6.96 us
  between operations: 13.8 us -> 0.12 us
    pallas_call x0 -> x2, Pallas kernels: none -> 594 us  [the longest x1 566 us: local_fused(): pl.pallas_call(functools.partial(kernel, p), out_shape=jax.ShapeDtypeStru...]
    all_to_all x1 -> x0, blocking collectives: 368 us -> none  [local(): lax.all_to_all(spread, ('ka', 'pb'), split_axis=0, concat_axis=0, tiled=T...]
    all_to_all x1 -> x0, waiting for transfers between devices: 198 us -> none  [local(): lax.all_to_all(leaving, ('ka', 'pb'), split_axis=0, concat_axis=0, tiled=...]
    dot_general x10 -> x0, matrix products: 130 us -> none  [the longest x1 24 us: local(): jnp.einsum('fbvdpl,dauplx->abfuvx', q_blocks, electron, precision=exact_m...]
    all_gather x1 -> x0, waiting for transfers between devices: 39 us -> none  [local(): gathered = lax.all_gather(gauge, 'ka', axis=1, tiled=True)]
    gather x2 -> x0, local copies, waits for them, and re-layouts: 34.6 us -> none  [local(): left_side = jnp.take(gathered, kq_index, axis=1)]
    reshape x2 -> x3, local copies, waits for them, and re-layouts: 33.6 us -> 0.92 us  [the longest x1 0.67 us: local_fused(): kq_index.reshape(-1)]
    another operation x2 -> x0, local copies, waits for them, and re-layouts: 17.6 us -> none  [rotate_gauge(): return jnp.stack([rot_real, rot_imag])]
  transfers between devices with their start and end apart: 2 -> 0, of which waited for: 2 -> 0; matrix products, arithmetic and copies ran while one was open for 4% -> 0% of each run, Pallas kernels for 0% -> 0%
where the time goes in v1:
time: 608 us; the launch traced here: 607 us
  Pallas kernels  594 us (98%)
  other arithmetic  6.96 us (1%)
    pallas_call x1, Pallas kernels, local_fused(): pl.pallas_call(functools.partial(kernel, p), out_shape=jax.ShapeDtypeStru...  566 us
    pallas_call x1, Pallas kernels, local_fused(): pl.pallas_call(functools.partial(unpack, p, step), grid=(p.re_local // st...  28.1 us

profile of v1, /device:TPU:9, one launch (start us, length us, event | category | flops | bytes accessed | tf_op | source)
XLA Modules:
  0.0 607.2 jit_solution(10066837118837499898)
XLA Ops:
  0.0 0.7 convert_element_type.26
  0.7 0.7 convert_element_type.23
  1.4 0.8 slice_bitcast_fusion.6
  2.2 0.7 broadcast_in_dim.13
  2.9 0.1 reshape.169
  3.0 0.8 copy.13
  3.8 0.7 reshape.167.kq
  4.5 0.1 broadcast_compare_fusion
  4.6 0.1 broadcast_in_dim.15
  4.7 0.1 convert_element_type.24
  4.8 0.4 multiply_divide_fusion.3
  5.3 0.8 pad_maximum_fusion.2.tk
  6.1 0.8 broadcast_in_dim.11
  6.9 0.0 copy-start
  6.9 0.1 reshape.168
  7.0 1.2 multiply_divide_fusion.1
  8.3 0.1 fusion.1
  8.4 1.1 pad_maximum_fusion.1.tq
  9.5 0.0 copy-done
  9.5 0.1 fusion.22
  9.6 0.4 slice_bitcast_fusion.1
  9.9 1.6 maximum_maximum_fusion.right
  11.6 0.1 pad_maximum_fusion
  11.7 1.3 copy.14.v_in
  13.0 566.1 %shard_map.82.x_ref = f32[8,4,1024,128]{3,2,1,0:T(8,128)} custom-call(f32[2,24,12,64,64]{4,3,2,1,0:T(8,128)} %bloch.1, f32[24,64,128]{2,1,0:T(8,128)} %copy.14.v_in, f32[24,128,128]{2,1,0:T(8,128)} %maximum_maximum_fusion.right, s32[288]{0:T(512)} %reshape.167.kq, bf16[512,576]{1,0:T(8,128)(2,1)} %pad_maximum_fusion.1.tq, bf16[256,288]{1,0:T(8,128)(2,1)} %pad_maximum_fusion.2.tk), custom_call_target="tpu_custom_call" | custom-call | tf_op jit(solution)/shard_map/pallas_call | solution.py:467
  579.1 28.1 %shard_map.83 = f32[2,32,16,64,64]{4,3,2,1,0:T(8,128)} custom-call(f32[8,4,1024,128]{3,2,1,0:T(8,128)} %shard_map.82.x_ref), custom_call_target="tpu_custom_call" | custom-call | tf_op jit(solution)/shard_map/pallas_call | solution.py:506
  (8 shorter events, 0.1 us)
Async XLA Ops:
  6.9 2.6 copy-start

commit v2 on v1

--- a/solution.py
+++ b/solution.py
@@ -120,7 +120,8 @@
         self.fits = (
             2 * bands == LANES
             and bands % self.devices == 0
-            and pb % 2 == 0
+            and pb & (pb - 1) == 0
+            and pb > 1
             and ka % 2 == 0
             and local_k % 6 == 0
         )
@@ -130,12 +131,13 @@
         self.share = self.rows * local_q
         self.kc = 3
         self.k_chunks = local_k // self.kc
-        self.rpc = 2
+        self.rpc = 1
         self.rp_chunks = self.rp_local // self.rpc
         self.width = self.rows * pb
         self.piece = self.rpc * self.rows * self.k_count
         self.block = self.re_local * self.rpc * self.width
-        self.slots = 2
+        self.slots = 4
+        self.ahead = 2
         self.fits = (
             self.share % 8 == 0
             and self.k_count % 16 == 0
@@ -184,6 +186,13 @@
     lane = lax.broadcasted_iota(jnp.int32, (1, LANES), 1)
     sign = jnp.where(lane < p.bands, 1.0, -1.0).astype(jnp.float32)
 
+    def partner(o):
+        t, bit = 0, 1
+        while bit < p.pb:
+            t = t + (b // bit + o // bit) % 2 * bit
+            bit *= 2
+        return t
+
     def load_g(k):
         return pltpu.make_async_copy(bloch.at[:, k], gbuf.at[k % 2], g_sem.at[k % 2])
 
@@ -263,15 +272,17 @@
             ) + dot(v_high, h_low)
         return carry
 
-    def send_1(c, o):
-        t = (me + o) % p.devices
+    def send_1(c, n):
+        ta = (a + p.ka - 1 - n % p.ka) % p.ka
+        tb = partner(p.pb - 1 - n // p.ka)
+        t = ta * p.pb + tb
         ks = pl.ds(c * p.kc, p.kc)
         return pltpu.make_async_remote_copy(
             src_ref=rot.at[ks, pl.ds(t * p.share, p.share)],
             dst_ref=x_buf.at[a, ks, b],
             send_sem=s1_sem.at[c],
             recv_sem=r1_sem.at[c],
-            device_id=(t // p.pb, t % p.pb),
+            device_id=(ta, tb),
             device_id_type=MESH,
         )
 
@@ -308,9 +319,9 @@
     def _(c):
         lax.fori_loop(c * p.kc, (c + 1) * p.kc, left_side, 0)
 
-        @pl.loop(1, p.devices)
-        def _(o):
-            send_1(c, o).start()
+        @pl.loop(0, p.devices - 1)
+        def _(n):
+            send_1(c, n).start()
 
         own_1(c).start()
 
@@ -321,7 +332,7 @@
     sum_q(p.k_chunks - 1)
 
     def send_2(j, o):
-        t = (b + o) % p.pb
+        t = partner(o)
         first = (t * p.rp_local + j * p.rpc) * p.rows * p.k_count
         return pltpu.make_async_remote_copy(
             src_ref=y_buf.at[pl.ds(first, p.piece)],
@@ -332,8 +343,7 @@
             device_id_type=MESH,
         )
 
-    @pl.loop(0, p.rp_chunks)
-    def _(j):
+    def start_2(j):
         @pl.loop(1, p.pb)
         def _(o):
             send_2(j, o).start()
@@ -342,6 +352,9 @@
         pltpu.make_async_copy(
             y_buf.at[pl.ds(first, p.piece)], z_buf.at[j, b], r2_sem.at[j]
         ).start()
+
+    for j in range(p.ahead):
+        start_2(j)
 
     def send_3(j, o):
         t = (a + o) % p.ka
@@ -369,6 +382,10 @@
     def _(j):
         pltpu.make_async_copy(z_buf.at[j], z_buf.at[j], r2_sem.at[j]).wait()
         slot = j % p.slots
+
+        @pl.when(j + p.ahead < p.rp_chunks)
+        def _():
+            start_2(j + p.ahead)
 
         @pl.when(j >= p.slots)
         def _():
@@ -484,7 +501,7 @@
             pltpu.VMEM((p.rp_count * p.rows * p.k_count, LANES), f32),
             pltpu.VMEM((p.rp_chunks, p.pb, p.piece, LANES), f32),
             pltpu.VMEM((p.slots, p.ka, p.block, LANES), f32),
-            dma((2,)),
+            dma((max(2, p.slots),)),
             dma,
             dma((p.ka,)),
             dma((p.ka,)),
@@ -502,7 +519,7 @@
         ),
     )(bloch, v_in, right, kq_index.reshape(-1), tq, tk)
 
-    step = 8
+    step = p.re_local
     return pl.pallas_call(
         functools.partial(unpack, p, step),
         grid=(p.re_local // step, p.rp_chunks),

time: 608 us -> 563 us (0.926)
  Pallas kernels: 594 us -> 549 us
    pallas_call x1, Pallas kernels: 566 us -> 529 us  [local_fused(): pl.pallas_call(functools.partial(kernel, p), out_shape=jax.ShapeDtypeStru...]
    pallas_call x1, Pallas kernels: 28.1 us -> 20.6 us  [local_fused(): pl.pallas_call(functools.partial(unpack, p, step), grid=(p.re_local // st...]
where the time goes in v2:
time: 563 us; the launch traced here: 562 us
  Pallas kernels  549 us (98%)
  other arithmetic  6.96 us (1%)
  local copies, waits for them, and re-layouts  5.96 us (1%)
    pallas_call x1, Pallas kernels, local_fused(): pl.pallas_call(functools.partial(kernel, p), out_shape=jax.ShapeDtypeStru...  529 us
    pallas_call x1, Pallas kernels, local_fused(): pl.pallas_call(functools.partial(unpack, p, step), grid=(p.re_local // st...  20.6 us

profile of v2, /device:TPU:9, one launch (start us, length us, event | category | flops | bytes accessed | tf_op | source)
XLA Modules:
  0.0 562.3 jit_solution(1681221051434198995)
XLA Ops:
  0.0 0.7 convert_element_type.26
  0.7 0.7 convert_element_type.23
  1.4 0.8 slice_bitcast_fusion.6
  2.2 0.7 broadcast_in_dim.13
  2.9 0.1 reshape.169
  3.0 0.8 copy.13
  3.8 0.7 reshape.167.kq
  4.5 0.1 broadcast_compare_fusion
  4.6 0.1 broadcast_in_dim.15
  4.7 0.1 convert_element_type.24
  4.8 0.4 multiply_divide_fusion.3
  5.3 0.8 pad_maximum_fusion.2.tk
  6.1 0.8 broadcast_in_dim.11
  6.9 0.0 copy-start
  6.9 0.1 reshape.168
  7.0 1.2 multiply_divide_fusion.1
  8.3 0.1 fusion.1
  8.4 1.1 pad_maximum_fusion.1.tq
  9.5 0.0 copy-done
  9.5 0.1 fusion.22
  9.6 0.4 slice_bitcast_fusion.1
  9.9 1.6 maximum_maximum_fusion.right
  11.6 0.1 pad_maximum_fusion
  11.7 1.3 copy.14.v_in
  13.0 528.7 %shard_map.82.x_ref = f32[16,4,512,128]{3,2,1,0:T(8,128)} custom-call(f32[2,24,12,64,64]{4,3,2,1,0:T(8,128)} %bloch.1, f32[24,64,128]{2,1,0:T(8,128)} %copy.14.v_in, f32[24,128,128]{2,1,0:T(8,128)} %maximum_maximum_fusion.right, s32[288]{0:T(512)} %reshape.167.kq, bf16[512,576]{1,0:T(8,128)(2,1)} %pad_maximum_fusion.1.tq, bf16[256,288]{1,0:T(8,128)(2,1)} %pad_maximum_fusion.2.tk), custom_call_target="tpu_custom_call" | custom-call | tf_op jit(solution)/shard_map/pallas_call | solution.py:484
  541.8 20.6 %shard_map.83 = f32[2,32,16,64,64]{4,3,2,1,0:T(8,128)} custom-call(f32[16,4,512,128]{3,2,1,0:T(8,128)} %shard_map.82.x_ref), custom_call_target="tpu_custom_call" | custom-call | tf_op jit(solution)/shard_map/pallas_call | solution.py:523
  (8 shorter events, 0.1 us)
Async XLA Ops:
  6.9 2.6 copy-start

commit v3 on v2

--- a/solution.py
+++ b/solution.py
@@ -111,7 +111,7 @@
 
 class Plan:
     def __init__(self, ka, pb, local_k, local_q, bands, re_count, rp_count):
-        self.ka, self.pb = ka, pb
+        self.ka, self.pb, self.half = ka, pb, pb // 2
         self.devices = ka * pb
         self.local_k, self.local_q, self.bands = local_k, local_q, bands
         self.k_count, self.q_count = ka * local_k, pb * local_q
@@ -121,30 +121,35 @@
             2 * bands == LANES
             and bands % self.devices == 0
             and pb & (pb - 1) == 0
-            and pb > 1
+            and pb > 2
             and ka % 2 == 0
             and local_k % 6 == 0
         )
         if not self.fits:
             return
+        self.kb = local_k // 3
+        self.kn = local_k - self.kb
+        self.kc = 2
+        self.steps = self.kb
         self.rows = bands // self.devices
         self.share = self.rows * local_q
-        self.kc = 3
-        self.k_chunks = local_k // self.kc
-        self.rpc = 1
-        self.rp_chunks = self.rp_local // self.rpc
+        self.wide = 2 * self.share
         self.width = self.rows * pb
-        self.piece = self.rpc * self.rows * self.k_count
-        self.block = self.re_local * self.rpc * self.width
-        self.slots = 4
+        self.piece = self.rows * ka * self.kn
+        self.sources = pb + self.half
+        self.block = self.re_local * self.width
+        self.raw_ahead = min(3, self.kb)
+        self.g_slots = 3
+        self.slots = 2
         self.ahead = 2
         self.fits = (
             self.share % 8 == 0
             and self.k_count % 16 == 0
+            and self.kb % 2 == 0
+            and (ka * self.kb) % 8 == 0
             and (pb * self.share) % 16 == 0
             and self.width % 8 == 0
-            and self.rp_local % self.rpc == 0
-            and self.rp_chunks > self.slots
+            and self.rp_local > self.slots
         )
 
 
@@ -154,13 +159,17 @@
     v_in,
     right,
     kq,
+    kq_far,
     tq,
+    tf,
     tk,
     out,
     gbuf,
     vg,
     rot,
+    far,
     x_buf,
+    xf_buf,
     y_buf,
     z_buf,
     w_buf,
@@ -170,8 +179,12 @@
     v1_sem,
     f_sem,
     v2_sem,
+    s0_sem,
+    r0_sem,
     s1_sem,
     r1_sem,
+    sf_sem,
+    rf_sem,
     s2_sem,
     r2_sem,
     s3_sem,
@@ -179,28 +192,33 @@
 ):
     a = lax.axis_index("ka")
     b = lax.axis_index("pb")
-    me = a * p.pb + b
     core = b % 2
     sibling = b + 1 - 2 * core
-    half = p.local_k // 2
+    side = b // p.half
+    seat = b % p.half
+    other = seat + (1 - side) * p.half
+    middle = p.local_k // 2
     lane = lax.broadcasted_iota(jnp.int32, (1, LANES), 1)
     sign = jnp.where(lane < p.bands, 1.0, -1.0).astype(jnp.float32)
 
-    def partner(o):
+    def xor(x, o, count):
         t, bit = 0, 1
-        while bit < p.pb:
-            t = t + (b // bit + o // bit) % 2 * bit
+        while bit < count:
+            t = t + (x // bit + o // bit) % 2 * bit
             bit *= 2
         return t
 
     def load_g(k):
-        return pltpu.make_async_copy(bloch.at[:, k], gbuf.at[k % 2], g_sem.at[k % 2])
-
-    load_g(0).start()
+        slot = k % p.g_slots
+        return pltpu.make_async_copy(bloch.at[:, k], gbuf.at[slot], g_sem.at[slot])
+
+    for k in range(p.g_slots):
+        load_g(k).start()
     own_v = pltpu.make_async_copy(v_in, vg.at[pl.ds(a * p.local_k, p.local_k)], own_sem)
     own_v.start()
 
     barrier = pltpu.get_barrier_semaphore()
+    me = a * p.pb + b
 
     @pl.loop(1, p.devices)
     def _(o):
@@ -211,8 +229,8 @@
 
     def send_v(i):
         return pltpu.make_async_remote_copy(
-            src_ref=v_in.at[pl.ds(core * half, half)],
-            dst_ref=vg.at[pl.ds(a * p.local_k + core * half, half)],
+            src_ref=v_in.at[pl.ds(core * middle, middle)],
+            dst_ref=vg.at[pl.ds(a * p.local_k + core * middle, middle)],
             send_sem=vs_sem.at[i],
             recv_sem=v1_sem.at[i],
             device_id=((a + i) % p.ka, b),
@@ -221,7 +239,7 @@
 
     def pass_v(i):
         source = (a + p.ka - i) % p.ka
-        part = pl.ds(source * p.local_k + core * half, half)
+        part = pl.ds(source * p.local_k + core * middle, middle)
         return pltpu.make_async_remote_copy(
             src_ref=vg.at[part],
             dst_ref=vg.at[part],
@@ -235,12 +253,8 @@
         send_v(i).start()
 
     def right_side(k, carry):
-        @pl.when(k + 1 < p.local_k)
-        def _():
-            load_g(k + 1).start()
-
         load_g(k).wait()
-        g = gbuf[k % 2]
+        g = gbuf[k % p.g_slots]
         g = jnp.concatenate([g[0], g[1]], axis=-1).reshape(p.local_q * p.bands, LANES)
         g_high, g_low = split(g)
         r_high, r_low = split(right[k])
@@ -250,36 +264,54 @@
         h = h.reshape(p.local_q, p.bands, LANES)
         for q in range(p.local_q):
             rot[k, pl.ds(q, p.bands, stride=p.local_q), :] = h[q]
+
+        @pl.when(k + p.g_slots < p.local_k)
+        def _():
+            load_g(k + p.g_slots).start()
+
         return carry
 
-    lax.fori_loop(0, half, right_side, 0)
+    def send_0(k):
+        return pltpu.make_async_remote_copy(
+            src_ref=rot.at[k],
+            dst_ref=far.at[k],
+            send_sem=s0_sem.at[k],
+            recv_sem=r0_sem.at[k],
+            device_id=(a, other),
+            device_id_type=MESH,
+        )
+
+    @pl.loop(0, p.raw_ahead)
+    def _(k):
+        right_side(k, 0)
+        send_0(k).start()
+
+    lax.fori_loop(p.raw_ahead, middle, right_side, 0)
     for i in range(1, p.ka):
         send_v(i).wait_recv()
         pass_v(i).start()
-    lax.fori_loop(half, p.local_k, right_side, 0)
+    lax.fori_loop(middle, p.local_k, right_side, 0)
     own_v.wait()
     for i in range(1, p.ka):
         pass_v(i).wait_recv()
 
-    def left_side(k, carry):
+    def left_side(buf, k, index, first):
         for q in range(p.local_q):
-            v_high, v_low = split(vg[kq[k * p.local_q + q]])
-            h = rot[k, pl.ds(q, p.bands, stride=p.local_q), :]
+            v_high, v_low = split(vg[index[first + q]])
+            h = buf[k, pl.ds(q, p.bands, stride=p.local_q), :]
             h_high, h_low = split(jnp.concatenate([h, swap(h, sign)], axis=0))
-            rot[k, pl.ds(q, p.bands, stride=p.local_q), :] = dot(
+            buf[k, pl.ds(q, p.bands, stride=p.local_q), :] = dot(
                 jnp.concatenate([v_high, v_low], axis=1),
                 jnp.concatenate([h_high, h_high], axis=0),
             ) + dot(v_high, h_low)
-        return carry
 
     def send_1(c, n):
         ta = (a + p.ka - 1 - n % p.ka) % p.ka
-        tb = partner(p.pb - 1 - n // p.ka)
+        tb = xor(b, p.pb - 1 - n // p.ka, p.pb)
         t = ta * p.pb + tb
-        ks = pl.ds(c * p.kc, p.kc)
         return pltpu.make_async_remote_copy(
-            src_ref=rot.at[ks, pl.ds(t * p.share, p.share)],
-            dst_ref=x_buf.at[a, ks, b],
+            src_ref=rot.at[pl.ds(p.kb + c * p.kc, p.kc), pl.ds(t * p.share, p.share)],
+            dst_ref=x_buf.at[a, pl.ds(c * p.kc, p.kc), b],
             send_sem=s1_sem.at[c],
             recv_sem=r1_sem.at[c],
             device_id=(ta, tb),
@@ -287,10 +319,40 @@
         )
 
     def own_1(c):
-        ks = pl.ds(c * p.kc, p.kc)
         return pltpu.make_async_copy(
-            rot.at[ks, pl.ds(me * p.share, p.share)], x_buf.at[a, ks, b], r1_sem.at[c]
-        )
+            rot.at[pl.ds(p.kb + c * p.kc, p.kc), pl.ds(me * p.share, p.share)],
+            x_buf.at[a, pl.ds(c * p.kc, p.kc), b],
+            r1_sem.at[c],
+        )
+
+    def send_f(buf, k, came_from, n):
+        ta = (a + p.ka - 1 - n % p.ka) % p.ka
+        ts = xor(seat, p.half - 1 - n // p.ka, p.half)
+        t = ta * p.half + ts
+        return pltpu.make_async_remote_copy(
+            src_ref=buf.at[k, pl.ds(t * p.wide, p.wide)],
+            dst_ref=xf_buf.at[a, k, came_from],
+            send_sem=sf_sem.at[k],
+            recv_sem=rf_sem.at[k],
+            device_id=(ta, side * p.half + ts),
+            device_id_type=MESH,
+        )
+
+    def own_f(buf, k, came_from):
+        t = a * p.half + seat
+        return pltpu.make_async_copy(
+            buf.at[k, pl.ds(t * p.wide, p.wide)], xf_buf.at[a, k, came_from], rf_sem.at[k]
+        )
+
+    def add_q(table, x, first, rows, stride, gap):
+        x_high, x_low = split(x)
+        y = dot(table[...], jnp.concatenate([x_high, x_high, x_low], axis=0))
+        for j in range(2):
+            cols = slice(j * LANES, (j + 1) * LANES)
+            where = pl.ds(first + j * gap, rows, stride=stride)
+            y_buf[where, :] = y[:rows, cols] + swap(y[rows:, cols], sign)
+
+    far_first = p.pb * p.rp_local * p.piece
 
     def sum_q(c):
         part = x_buf.at[:, pl.ds(c * p.kc, p.kc)]
@@ -307,17 +369,34 @@
                 ],
                 axis=1,
             )
-            x_high, x_low = split(x)
-            y = dot(tq[...], jnp.concatenate([x_high, x_high, x_low], axis=0))
-            rows = p.rp_count * p.rows
-            for j in range(2):
-                cols = slice(j * LANES, (j + 1) * LANES)
-                where = pl.ds((2 * pair + j) * p.local_k + k, rows, stride=p.k_count)
-                y_buf[where, :] = y[:rows, cols] + swap(y[rows:, cols], sign)
-
-    @pl.loop(0, p.k_chunks)
+            add_q(tq, x, 2 * pair * p.kn + k, p.rp_count * p.rows, p.ka * p.kn, p.kn)
+
+        part = xf_buf.at[:, pl.ds(c, 1)]
+        pltpu.make_async_copy(part, part, rf_sem.at[c]).wait()
+
+        @pl.loop(0, p.ka // 2)
+        def _(pair):
+            x = jnp.concatenate(
+                [
+                    xf_buf[2 * pair, c].reshape(p.pb * p.wide, LANES),
+                    xf_buf[2 * pair + 1, c].reshape(p.pb * p.wide, LANES),
+                ],
+                axis=1,
+            )
+            add_q(
+                tf,
+                x,
+                far_first + 2 * pair * p.kb + c,
+                p.rp_count * p.rows,
+                p.ka * p.kb,
+                p.kb,
+            )
+
+    @pl.loop(0, p.steps)
     def _(c):
-        lax.fori_loop(c * p.kc, (c + 1) * p.kc, left_side, 0)
+        @pl.loop(c * p.kc, (c + 1) * p.kc)
+        def _(k):
+            left_side(rot, p.kb + k, kq, (p.kb + k) * p.local_q)
 
         @pl.loop(0, p.devices - 1)
         def _(n):
@@ -325,17 +404,37 @@
 
         own_1(c).start()
 
+        @pl.when(c + p.raw_ahead < p.kb)
+        def _():
+            send_0(c + p.raw_ahead).start()
+
+        send_0(c).wait_send()
+        left_side(rot, c, kq, c * p.local_q)
+
+        @pl.loop(0, p.ka * p.half - 1)
+        def _(n):
+            send_f(rot, c, b, n).start()
+
+        own_f(rot, c, b).start()
+        send_0(c).wait_recv()
+        left_side(far, c, kq_far, c * p.local_q)
+
+        @pl.loop(0, p.ka * p.half - 1)
+        def _(n):
+            send_f(far, c, other, n).start()
+
+        own_f(far, c, other).start()
+
         @pl.when(c > 0)
         def _():
             sum_q(c - 1)
 
-    sum_q(p.k_chunks - 1)
+    sum_q(p.steps - 1)
 
     def send_2(j, o):
-        t = partner(o)
-        first = (t * p.rp_local + j * p.rpc) * p.rows * p.k_count
+        t = xor(b, o, p.pb)
         return pltpu.make_async_remote_copy(
-            src_ref=y_buf.at[pl.ds(first, p.piece)],
+            src_ref=y_buf.at[pl.ds((t * p.rp_local + j) * p.piece, p.piece)],
             dst_ref=z_buf.at[j, b],
             send_sem=s2_sem.at[j],
             recv_sem=r2_sem.at[j],
@@ -343,15 +442,32 @@
             device_id_type=MESH,
         )
 
+    def send_2f(j, o):
+        t = xor(seat, o, p.half)
+        return pltpu.make_async_remote_copy(
+            src_ref=y_buf.at[pl.ds(((p.pb + t) * p.rp_local + j) * p.piece, p.piece)],
+            dst_ref=z_buf.at[j, p.pb + seat],
+            send_sem=s2_sem.at[j],
+            recv_sem=r2_sem.at[j],
+            device_id=(a, side * p.half + t),
+            device_id_type=MESH,
+        )
+
     def start_2(j):
         @pl.loop(1, p.pb)
         def _(o):
             send_2(j, o).start()
 
-        first = (b * p.rp_local + j * p.rpc) * p.rows * p.k_count
-        pltpu.make_async_copy(
-            y_buf.at[pl.ds(first, p.piece)], z_buf.at[j, b], r2_sem.at[j]
-        ).start()
+        @pl.loop(1, p.half)
+        def _(o):
+            send_2f(j, o).start()
+
+        for mine in (b, p.pb + seat):
+            pltpu.make_async_copy(
+                y_buf.at[pl.ds((mine * p.rp_local + j) * p.piece, p.piece)],
+                z_buf.at[j, mine],
+                r2_sem.at[j],
+            ).start()
 
     for j in range(p.ahead):
         start_2(j)
@@ -378,12 +494,14 @@
         pltpu.make_async_copy(sent, sent, s3_sem.at[slot]).wait()
         own_3(j).wait()
 
-    @pl.loop(0, p.rp_chunks)
+    near, less = p.ka * p.kn, p.ka * p.kb
+
+    @pl.loop(0, p.rp_local)
     def _(j):
         pltpu.make_async_copy(z_buf.at[j], z_buf.at[j], r2_sem.at[j]).wait()
         slot = j % p.slots
 
-        @pl.when(j + p.ahead < p.rp_chunks)
+        @pl.when(j + p.ahead < p.rp_local)
         def _():
             start_2(j + p.ahead)
 
@@ -391,15 +509,24 @@
         def _():
             free_3(j - p.slots)
 
-        @pl.loop(0, p.pb * p.rpc)
-        def _(i):
-            source = i // p.rpc
-            rp = i % p.rpc
+        @pl.loop(0, p.pb)
+        def _(source):
             for r in range(0, p.rows, 2):
                 z = jnp.concatenate(
                     [
-                        z_buf[j, source, pl.ds((rp * p.rows + r) * p.k_count, p.k_count), :],
-                        z_buf[j, source, pl.ds((rp * p.rows + r + 1) * p.k_count, p.k_count), :],
+                        jnp.concatenate(
+                            [
+                                z_buf[j, source, (r + s) * near : (r + s + 1) * near, :],
+                                z_buf[
+                                    j,
+                                    p.pb + source // 2,
+                                    pl.ds((source % 2 * p.rows + r + s) * less, less),
+                                    :,
+                                ],
+                            ],
+                            axis=0,
+                        )
+                        for s in range(2)
                     ],
                     axis=1,
                 )
@@ -408,8 +535,7 @@
                 for s in range(2):
                     cols = slice(s * LANES, (s + 1) * LANES)
                     full = w[: p.re_count, cols] + swap(w[p.re_count :, cols], sign)
-                    at = rp * p.width + source * p.rows + r + s
-                    where = pl.ds(at, p.re_local, stride=p.rpc * p.width)
+                    where = pl.ds(source * p.rows + r + s, p.re_local, stride=p.width)
                     for t in range(p.ka):
                         w_buf[slot, t, where, :] = full[t * p.re_local : (t + 1) * p.re_local]
 
@@ -419,20 +545,22 @@
 
         own_3(j).start()
 
-    for j in range(p.rp_chunks - p.slots, p.rp_chunks):
+    for j in range(p.rp_local - p.slots, p.rp_local):
         free_3(j)
 
-    @pl.loop(0, p.rp_chunks)
+    @pl.loop(0, p.rp_local)
     def _(j):
         into = out.at[j, pl.ds(0, p.ka - 1)]
         pltpu.make_async_copy(into, into, r3_sem.at[j]).wait()
-        first = z_buf.at[j, pl.ds(0, p.pb - 1)]
-        pltpu.make_async_copy(first, first, s2_sem.at[j]).wait()
-
-    @pl.loop(0, p.k_chunks)
+        sent = z_buf.at[j, pl.ds(0, p.sources - 2)]
+        pltpu.make_async_copy(sent, sent, s2_sem.at[j]).wait()
+
+    @pl.loop(0, p.steps)
     def _(c):
         sent = rot.at[pl.ds(c * p.kc, p.kc), pl.ds(0, (p.devices - 1) * p.share)]
         pltpu.make_async_copy(sent, sent, s1_sem.at[c]).wait()
+        sent = rot.at[pl.ds(c, 2), pl.ds(0, (p.ka * p.half - 1) * p.wide)]
+        pltpu.make_async_copy(sent, sent, sf_sem.at[c]).wait()
 
     for i in range(1, p.ka):
         send_v(i).wait_send()
@@ -441,7 +569,7 @@
 
 def unpack(p, step, x_ref, o_ref):
     for t in range(p.ka):
-        x = x_ref[0, t].reshape(step, p.rpc, p.width, LANES)
+        x = x_ref[0, t].reshape(step, 1, p.width, LANES)
         o_ref[0, :, :, t * p.width : (t + 1) * p.width, :] = x[..., : p.bands]
         o_ref[1, :, :, t * p.width : (t + 1) * p.width, :] = x[..., p.bands :]
 
@@ -458,79 +586,100 @@
     right = jnp.concatenate(
         [jnp.concatenate([real, imag], axis=2), jnp.concatenate([-imag, real], axis=2)], axis=1
     )
-    vectors = jnp.repeat(rp_vectors, p.rows, axis=0)
-    points = jnp.broadcast_to(
-        qpoint.reshape(p.pb, 1, p.local_q), (p.pb, p.rows, p.local_q)
-    ).reshape(-1)
-    cosine, sine = mesh_phase(vectors, points, p.q_count)
-    row = jnp.arange(p.rp_count * p.rows, dtype=jnp.int32) % p.rows
-    col = jnp.arange(p.q_count * p.rows, dtype=jnp.int32) // p.local_q % p.rows
-    weight = jnp.repeat(rp_weight, p.rows).astype(jnp.float32)[:, None]
-    same = row[:, None] == col[None, :]
-    tq = jnp.where(
-        jnp.concatenate([same, same], axis=0),
-        jnp.concatenate([cosine / weight, sine / weight], axis=0),
-        0.0,
-    )
-    cosine, sine = mesh_phase(re_vectors, jnp.arange(p.k_count, dtype=jnp.int32), p.k_count)
+    a, b = lax.axis_index("ka"), lax.axis_index("pb")
+    slots = qpoint.reshape(p.pb, p.local_q)
+    other = (b + p.half) % p.pb
+    far_q = lax.dynamic_index_in_dim(slots, other, 0, keepdims=True)
+    far_k = (a * p.local_k + jnp.arange(p.kb, dtype=jnp.int32))[:, None]
+    first = (far_k // (MK2 * MK3) + far_q // (MK2 * MK3)) % MK1
+    second = (far_k // MK3 % MK2 + far_q // MK3 % MK2) % MK2
+    third = (far_k % MK3 + far_q % MK3) % MK3
+    kq_far = (first * MK2 + second) * MK3 + third
+
+    def q_table(vectors, weight, rows):
+        vectors = jnp.repeat(vectors, rows, axis=0)
+        points = jnp.broadcast_to(slots[:, None, :], (p.pb, rows, p.local_q)).reshape(-1)
+        cosine, sine = mesh_phase(vectors, points, p.q_count)
+        row = jnp.arange(vectors.shape[0], dtype=jnp.int32) % rows
+        col = jnp.arange(points.shape[0], dtype=jnp.int32) // p.local_q % rows
+        weight = jnp.repeat(weight, rows).astype(jnp.float32)[:, None]
+        same = row[:, None] == col[None, :]
+        return three_parts(
+            jnp.where(
+                jnp.concatenate([same, same], axis=0),
+                jnp.concatenate([cosine / weight, sine / weight], axis=0),
+                0.0,
+            )
+        )
+
+    tq = q_table(rp_vectors, rp_weight, p.rows)
+    near = p.rp_count // 2
+    start = b // p.half * near
+    tf = q_table(
+        lax.dynamic_slice_in_dim(rp_vectors, start, near),
+        lax.dynamic_slice_in_dim(rp_weight, start, near),
+        2 * p.rows,
+    )
+    points = jnp.arange(p.k_count, dtype=jnp.int32).reshape(p.ka, p.local_k)
+    points = jnp.concatenate([points[:, p.kb :].reshape(-1), points[:, : p.kb].reshape(-1)])
+    cosine, sine = mesh_phase(re_vectors, points, p.k_count)
     weight = re_weight.astype(jnp.float32)[:, None]
-    tk = jnp.concatenate([cosine / weight, sine / weight], axis=0)
-    tq, tk = three_parts(tq), three_parts(tk)
+    tk = three_parts(jnp.concatenate([cosine / weight, sine / weight], axis=0))
 
     f32 = jnp.float32
     dma = pltpu.SemaphoreType.DMA
     vmem = pl.BlockSpec(memory_space=pltpu.VMEM)
     any_space = pl.BlockSpec(memory_space=pl.ANY)
+    smem = pl.BlockSpec(memory_space=pltpu.SMEM)
     landed = pl.pallas_call(
         functools.partial(kernel, p),
-        out_shape=jax.ShapeDtypeStruct((p.rp_chunks, p.ka, p.block, LANES), f32),
-        in_specs=[
-            any_space,
-            any_space,
-            vmem,
-            pl.BlockSpec(memory_space=pltpu.SMEM),
-            vmem,
-            vmem,
-        ],
+        out_shape=jax.ShapeDtypeStruct((p.rp_local, p.ka, p.block, LANES), f32),
+        in_specs=[any_space, any_space, vmem, smem, smem, vmem, vmem, vmem],
         out_specs=any_space,
         scratch_shapes=[
-            pltpu.VMEM((2, 2, p.local_q, p.bands, p.bands), f32),
+            pltpu.VMEM((p.g_slots, 2, p.local_q, p.bands, p.bands), f32),
             pltpu.VMEM((p.k_count, p.bands, LANES), f32),
             pltpu.VMEM((p.local_k, p.devices * p.share, LANES), f32),
-            pltpu.VMEM((p.ka, p.local_k, p.pb, p.share, LANES), f32),
-            pltpu.VMEM((p.rp_count * p.rows * p.k_count, LANES), f32),
-            pltpu.VMEM((p.rp_chunks, p.pb, p.piece, LANES), f32),
+            pltpu.VMEM((p.kb, p.devices * p.share, LANES), f32),
+            pltpu.VMEM((p.ka, p.kn, p.pb, p.share, LANES), f32),
+            pltpu.VMEM((p.ka, p.kb, p.pb, p.wide, LANES), f32),
+            pltpu.VMEM((p.sources * p.rp_local * p.piece, LANES), f32),
+            pltpu.VMEM((p.rp_local, p.sources, p.piece, LANES), f32),
             pltpu.VMEM((p.slots, p.ka, p.block, LANES), f32),
-            dma((max(2, p.slots),)),
+            dma((max(p.g_slots, p.slots),)),
             dma,
             dma((p.ka,)),
             dma((p.ka,)),
             dma((p.ka,)),
             dma((p.ka,)),
-            dma((p.k_chunks,)),
-            dma((p.k_chunks,)),
-            dma((p.rp_chunks,)),
-            dma((p.rp_chunks,)),
+            dma((p.kb,)),
+            dma((p.kb,)),
+            dma((p.steps,)),
+            dma((p.steps,)),
+            dma((p.kb,)),
+            dma((p.kb,)),
+            dma((p.rp_local,)),
+            dma((p.rp_local,)),
             dma((p.slots,)),
-            dma((p.rp_chunks,)),
+            dma((p.rp_local,)),
         ],
         compiler_params=pltpu.CompilerParams(
             collective_id=0, has_side_effects=True, vmem_limit_bytes=VMEM_BYTES
         ),
-    )(bloch, v_in, right, kq_index.reshape(-1), tq, tk)
+    )(bloch, v_in, right, kq_index.reshape(-1), kq_far.reshape(-1), tq, tf, tk)
 
     step = p.re_local
     return pl.pallas_call(
         functools.partial(unpack, p, step),
-        grid=(p.re_local // step, p.rp_chunks),
+        grid=(p.re_local // step, p.rp_local),
         out_shape=jax.ShapeDtypeStruct((2, p.re_local, p.rp_local, p.bands, p.bands), f32),
         in_specs=[
             pl.BlockSpec(
-                (1, p.ka, step * p.rpc * p.width, LANES), lambda i, j: (j, 0, i, 0)
+                (1, p.ka, step * p.width, LANES), lambda i, j: (j, 0, i, 0)
             )
         ],
         out_specs=pl.BlockSpec(
-            (2, step, p.rpc, p.bands, p.bands), lambda i, j: (0, i, j, 0, 0)
+            (2, step, 1, p.bands, p.bands), lambda i, j: (0, i, j, 0, 0)
         ),
     )(landed)
 

time: 563 us -> 534 us (0.948)
  Pallas kernels: 549 us -> 513 us
    pallas_call x1, Pallas kernels: 529 us -> 492 us  [local_fused(): pl.pallas_call(functools.partial(kernel, p), out_shape=jax.ShapeDtypeStru...]
where the time goes in v3:
time: 534 us; the launch traced here: 533 us
  Pallas kernels  513 us (96%)
  other arithmetic  12 us (2%)
  local copies, waits for them, and re-layouts  7.57 us (1%)
    pallas_call x1, Pallas kernels, local_fused(): pl.pallas_call(functools.partial(kernel, p), out_shape=jax.ShapeDtypeStru...  492 us
    pallas_call x1, Pallas kernels, local_fused(): pl.pallas_call(functools.partial(unpack, p, step), grid=(p.re_local // st...  20.6 us

profile of v3, /device:TPU:9, one launch (start us, length us, event | category | flops | bytes accessed | tf_op | source)
XLA Modules:
  0.0 532.8 jit_solution(9197051576644943087)
XLA Ops:
  0.0 0.0 copy-start.1
  0.0 0.7 convert_element_type.44
  0.7 0.7 dynamic-slice_convert_fusion
  1.4 0.7 convert_element_type.38
  2.1 0.8 constant_dynamic-slice_fusion
  2.9 0.8 slice_bitcast_fusion.6
  3.7 0.1 concatenate.89
  3.8 0.1 slice.48
  3.9 0.1 concatenate.88
  3.9 0.1 fusion.45
  4.1 0.7 reshape.524
  4.8 0.1 broadcast_add_fusion
  4.9 0.1 add.354
  5.0 0.1 add_remainder_fusion.3
  5.1 0.1 rem.450
  5.2 0.1 broadcast_add_fusion.1
  5.2 0.1 add.338
  5.3 0.6 fusion.35.kq_far
  5.9 0.1 reshape.526
  6.1 0.1 reshape.528
  6.2 0.8 copy.14
  7.0 0.7 reshape.523.kq
  7.7 0.1 broadcast_in_dim.25
  7.7 0.1 convert_element_type.42
  7.9 0.1 broadcast_compare_fusion.1
  8.0 0.1 broadcast_in_dim.21
  8.0 0.1 convert_element_type.39
  8.2 0.1 broadcast_compare_fusion
  8.3 0.1 broadcast_in_dim.23
  8.4 0.1 reshape.527
  8.5 0.4 multiply_divide_fusion.5
  9.0 0.8 pad_maximum_fusion.3.tk
  9.8 0.0 copy-done.1
  9.8 0.1 broadcast_in_dim.19
  9.9 0.2 reshape.525
  10.1 1.2 multiply_divide_fusion.3
  11.3 0.1 fusion.3
  11.5 1.1 pad_maximum_fusion.2.tq
  12.5 1.8 multiply_divide_fusion.1
  14.3 0.0 copy-start
  14.4 0.2 fusion.1
  14.5 1.1 pad_maximum_fusion.1.tf
  15.7 0.5 copy-done
  16.2 0.1 fusion.46
  16.3 0.4 slice_bitcast_fusion.1
  16.6 1.6 maximum_maximum_fusion.right
  18.3 0.1 pad_maximum_fusion
  18.4 1.4 copy.15.v_in
  19.7 492.5 %shard_map.82.x_ref = f32[16,4,512,128]{3,2,1,0:T(8,128)} custom-call(f32[2,24,12,64,64]{4,3,2,1,0:T(8,128)} %bloch.1, f32[24,64,128]{2,1,0:T(8,128)} %copy.15.v_in, f32[24,128,128]{2,1,0:T(8,128)} %maximum_maximum_fusion.right, s32[288]{0:T(512)} %reshape.523.kq, s32[96]{0:T(128)} %fusion.35.kq_far, bf16[512,576]{1,0:T(8,128)(2,1)} %pad_maximum_fusion.2.tq, ...), custom_call_target="tpu_custom_call" | custom-call | tf_op jit(solution)/shard_map/pallas_call | solution.py:634
  512.2 20.6 %shard_map.83 = f32[2,32,16,64,64]{4,3,2,1,0:T(8,128)} custom-call(f32[16,4,512,128]{3,2,1,0:T(8,128)} %shard_map.82.x_ref), custom_call_target="tpu_custom_call" | custom-call | tf_op jit(solution)/shard_map/pallas_call | solution.py:672
  (17 shorter events, 0.2 us)
Async XLA Ops:
  0.0 9.8 %copy-start.1 = (s32[128,3]{0,1:T(4,128)S(1)}, s32[128,3]{0,1:T(4,128)}, u32[]{:S(2)}) copy-start(s32[128,3]{0,1:T(4,128)} %param.14) | copy-start | bytes 4612
  14.3 1.8 copy-start

commit v4 on v3

--- a/solution.py
+++ b/solution.py
@@ -129,8 +129,6 @@
             return
         self.kb = local_k // 3
         self.kn = local_k - self.kb
-        self.kc = 2
-        self.steps = self.kb
         self.rows = bands // self.devices
         self.share = self.rows * local_q
         self.wide = 2 * self.share
@@ -153,17 +151,89 @@
         )
 
 
+def digits(point):
+    return point // (MK2 * MK3), point // MK3 % MK2, point % MK3
+
+
+def phases(columns, points, count):
+    first, second, third = (d.astype(jnp.float32) for d in digits(points))
+    total = MK1 * MK2 * MK3
+    turns = (
+        columns[:, 0:1] * (first * (MK2 * MK3))
+        + columns[:, 1:2] * (second * (MK1 * MK3))
+        + columns[:, 2:3] * (third * (MK1 * MK2))
+    )
+    turns = turns - total * jnp.floor((turns + 0.5) / total)
+    angles = turns * (2.0 * math.pi / total)
+    weight = columns[:, 3:4]
+    return jnp.cos(angles) / count / weight, jnp.sin(angles) / count / weight
+
+
+def pick(rows, values):
+    source = lax.broadcasted_iota(jnp.int32, (rows.shape[0], values.shape[1]), 1)
+    chosen = jnp.where(rows == source, 1.0, 0.0).astype(jnp.bfloat16)
+    return lax.dot_general(
+        chosen,
+        values.astype(jnp.bfloat16),
+        (((1,), (1,)), ((), ())),
+        preferred_element_type=jnp.float32,
+    )
+
+
+def put_table(table, real, imag):
+    full = jnp.concatenate([real, imag], axis=0)
+    high, low = split(full)
+    high = high.astype(jnp.float32)
+    full = jnp.concatenate([high, low.astype(jnp.float32), high], axis=1)
+    table[...] = full.astype(jnp.bfloat16)
+
+
+def make_tables(p, side, slots, vectors, weights, tq, tf, tk):
+    f32 = jnp.float32
+    iota = lambda shape, dim: lax.broadcasted_iota(jnp.int32, shape, dim)
+    rp = jnp.concatenate([vectors[3:6], weights[1:2]], axis=0).astype(f32)
+    re = jnp.concatenate([vectors[0:3], weights[0:1]], axis=0).astype(f32)
+
+    def q_table(table, start, count, rows):
+        row = iota((count * rows, 1), 0)
+        columns = pick(start + row // rows, rp)
+        width = rows * p.q_count
+        col = iota((1, width), 1)
+        slot = col // (rows * p.local_q) * p.local_q + col % p.local_q
+        chosen = jnp.where(iota((p.q_count, width), 0) == slot, 1.0, 0.0)
+        held = jnp.broadcast_to(slots[...], (8, p.q_count)).astype(f32)
+        points = dot(held.astype(jnp.bfloat16), chosen.astype(jnp.bfloat16))[0:1]
+        cosine, sine = phases(columns, points.astype(jnp.int32), p.q_count)
+        same = row % rows == col // p.local_q % rows
+        put_table(table, jnp.where(same, cosine, 0.0), jnp.where(same, sine, 0.0))
+
+    q_table(tq, 0, p.rp_count, p.rows)
+    q_table(tf, side * (p.rp_count // 2), p.rp_count // 2, 2 * p.rows)
+
+    columns = pick(iota((p.re_count, 1), 0), re)
+    col = iota((1, p.k_count), 1)
+    near = p.ka * p.kn
+    point = jnp.where(
+        col < near,
+        col // p.kn * p.local_k + p.kb + col % p.kn,
+        (col - near) // p.kb * p.local_k + (col - near) % p.kb,
+    )
+    cosine, sine = phases(columns, point, p.k_count)
+    put_table(tk, cosine, sine)
+
+
 def kernel(
     p,
     bloch,
-    v_in,
-    right,
-    kq,
-    kq_far,
+    gauge,
+    qpoint,
+    slots,
+    vectors,
+    weights,
+    out,
     tq,
     tf,
     tk,
-    out,
     gbuf,
     vg,
     rot,
@@ -174,7 +244,6 @@
     z_buf,
     w_buf,
     g_sem,
-    own_sem,
     vs_sem,
     v1_sem,
     f_sem,
@@ -214,8 +283,6 @@
 
     for k in range(p.g_slots):
         load_g(k).start()
-    own_v = pltpu.make_async_copy(v_in, vg.at[pl.ds(a * p.local_k, p.local_k)], own_sem)
-    own_v.start()
 
     barrier = pltpu.get_barrier_semaphore()
     me = a * p.pb + b
@@ -225,11 +292,17 @@
         t = (me + o) % p.devices
         pl.semaphore_signal(barrier, inc=1, device_id=(t // p.pb, t % p.pb), device_id_type=MESH)
 
+    @pl.loop(0, p.local_k)
+    def _(k):
+        vg[a * p.local_k + k] = jnp.concatenate(
+            [jnp.transpose(gauge[0, k]), jnp.transpose(gauge[1, k])], axis=1
+        )
+
     pl.semaphore_wait(barrier, p.devices - 1)
 
     def send_v(i):
         return pltpu.make_async_remote_copy(
-            src_ref=v_in.at[pl.ds(core * middle, middle)],
+            src_ref=vg.at[pl.ds(a * p.local_k + core * middle, middle)],
             dst_ref=vg.at[pl.ds(a * p.local_k + core * middle, middle)],
             send_sem=vs_sem.at[i],
             recv_sem=v1_sem.at[i],
@@ -257,7 +330,12 @@
         g = gbuf[k % p.g_slots]
         g = jnp.concatenate([g[0], g[1]], axis=-1).reshape(p.local_q * p.bands, LANES)
         g_high, g_low = split(g)
-        r_high, r_low = split(right[k])
+        u, v = gauge[0, k], gauge[1, k]
+        r_high, r_low = split(
+            jnp.concatenate(
+                [jnp.concatenate([u, v], axis=1), jnp.concatenate([-v, u], axis=1)], axis=0
+            )
+        )
         h = dot(
             jnp.concatenate([g_high, g_low], axis=1), jnp.concatenate([r_high, r_high], axis=0)
         ) + dot(g_high, r_low)
@@ -287,20 +365,23 @@
         send_0(k).start()
 
     lax.fori_loop(p.raw_ahead, middle, right_side, 0)
+    make_tables(p, side, slots, vectors, weights, tq, tf, tk)
     for i in range(1, p.ka):
         send_v(i).wait_recv()
         pass_v(i).start()
     lax.fori_loop(middle, p.local_k, right_side, 0)
-    own_v.wait()
     for i in range(1, p.ka):
         pass_v(i).wait_recv()
 
-    def left_side(buf, k, index, first):
+    def left_side(buf, row, k, source):
+        k1, k2, k3 = digits(a * p.local_k + k)
         for q in range(p.local_q):
-            v_high, v_low = split(vg[index[first + q]])
-            h = buf[k, pl.ds(q, p.bands, stride=p.local_q), :]
+            q1, q2, q3 = digits(qpoint[source * p.local_q + q])
+            kq = ((k1 + q1) % MK1 * MK2 + (k2 + q2) % MK2) * MK3 + (k3 + q3) % MK3
+            v_high, v_low = split(vg[kq])
+            h = buf[row, pl.ds(q, p.bands, stride=p.local_q), :]
             h_high, h_low = split(jnp.concatenate([h, swap(h, sign)], axis=0))
-            buf[k, pl.ds(q, p.bands, stride=p.local_q), :] = dot(
+            buf[row, pl.ds(q, p.bands, stride=p.local_q), :] = dot(
                 jnp.concatenate([v_high, v_low], axis=1),
                 jnp.concatenate([h_high, h_high], axis=0),
             ) + dot(v_high, h_low)
@@ -310,8 +391,8 @@
         tb = xor(b, p.pb - 1 - n // p.ka, p.pb)
         t = ta * p.pb + tb
         return pltpu.make_async_remote_copy(
-            src_ref=rot.at[pl.ds(p.kb + c * p.kc, p.kc), pl.ds(t * p.share, p.share)],
-            dst_ref=x_buf.at[a, pl.ds(c * p.kc, p.kc), b],
+            src_ref=rot.at[p.kb + c, pl.ds(t * p.share, p.share)],
+            dst_ref=x_buf.at[a, c, b],
             send_sem=s1_sem.at[c],
             recv_sem=r1_sem.at[c],
             device_id=(ta, tb),
@@ -320,9 +401,7 @@
 
     def own_1(c):
         return pltpu.make_async_copy(
-            rot.at[pl.ds(p.kb + c * p.kc, p.kc), pl.ds(me * p.share, p.share)],
-            x_buf.at[a, pl.ds(c * p.kc, p.kc), b],
-            r1_sem.at[c],
+            rot.at[p.kb + c, pl.ds(me * p.share, p.share)], x_buf.at[a, c, b], r1_sem.at[c]
         )
 
     def send_f(buf, k, came_from, n):
@@ -354,23 +433,22 @@
 
     far_first = p.pb * p.rp_local * p.piece
 
-    def sum_q(c):
-        part = x_buf.at[:, pl.ds(c * p.kc, p.kc)]
+    def sum_near(c):
+        part = x_buf.at[:, pl.ds(c, 1)]
         pltpu.make_async_copy(part, part, r1_sem.at[c]).wait()
 
-        @pl.loop(0, (p.ka // 2) * p.kc)
-        def _(i):
-            pair = i // p.kc
-            k = c * p.kc + i % p.kc
+        @pl.loop(0, p.ka // 2)
+        def _(pair):
             x = jnp.concatenate(
                 [
-                    x_buf[2 * pair, k].reshape(p.pb * p.share, LANES),
-                    x_buf[2 * pair + 1, k].reshape(p.pb * p.share, LANES),
+                    x_buf[2 * pair, c].reshape(p.pb * p.share, LANES),
+                    x_buf[2 * pair + 1, c].reshape(p.pb * p.share, LANES),
                 ],
                 axis=1,
             )
-            add_q(tq, x, 2 * pair * p.kn + k, p.rp_count * p.rows, p.ka * p.kn, p.kn)
-
+            add_q(tq, x, 2 * pair * p.kn + c, p.rp_count * p.rows, p.ka * p.kn, p.kn)
+
+    def sum_far(c):
         part = xf_buf.at[:, pl.ds(c, 1)]
         pltpu.make_async_copy(part, part, rf_sem.at[c]).wait()
 
@@ -392,44 +470,48 @@
                 p.kb,
             )
 
-    @pl.loop(0, p.steps)
+    def begin(c):
+        return c * c * p.kn // (p.kb * p.kb)
+
+    @pl.loop(0, p.kb + 1)
     def _(c):
-        @pl.loop(c * p.kc, (c + 1) * p.kc)
-        def _(k):
-            left_side(rot, p.kb + k, kq, (p.kb + k) * p.local_q)
-
-        @pl.loop(0, p.devices - 1)
-        def _(n):
-            send_1(c, n).start()
-
-        own_1(c).start()
-
-        @pl.when(c + p.raw_ahead < p.kb)
+        @pl.when(c < p.kb)
         def _():
-            send_0(c + p.raw_ahead).start()
-
-        send_0(c).wait_send()
-        left_side(rot, c, kq, c * p.local_q)
-
-        @pl.loop(0, p.ka * p.half - 1)
-        def _(n):
-            send_f(rot, c, b, n).start()
-
-        own_f(rot, c, b).start()
-        send_0(c).wait_recv()
-        left_side(far, c, kq_far, c * p.local_q)
-
-        @pl.loop(0, p.ka * p.half - 1)
-        def _(n):
-            send_f(far, c, other, n).start()
-
-        own_f(far, c, other).start()
+            send_0(c).wait_send()
+            left_side(rot, c, c, b)
+
+            @pl.loop(0, p.ka * p.half - 1)
+            def _(n):
+                send_f(rot, c, b, n).start()
+
+            own_f(rot, c, b).start()
+            send_0(c).wait_recv()
+            left_side(far, c, c, other)
+
+            @pl.loop(0, p.ka * p.half - 1)
+            def _(n):
+                send_f(far, c, other, n).start()
+
+            own_f(far, c, other).start()
+
+            @pl.loop(begin(c), begin(c + 1))
+            def _(k):
+                left_side(rot, p.kb + k, p.kb + k, b)
+
+                @pl.loop(0, p.devices - 1)
+                def _(n):
+                    send_1(k, n).start()
+
+                own_1(k).start()
+
+            @pl.when(c + p.raw_ahead < p.kb)
+            def _():
+                send_0(c + p.raw_ahead).start()
 
         @pl.when(c > 0)
         def _():
-            sum_q(c - 1)
-
-    sum_q(p.steps - 1)
+            sum_far(c - 1)
+            pl.loop(begin(c - 1), begin(c))(sum_near)
 
     def send_2(j, o):
         t = xor(b, o, p.pb)
@@ -555,10 +637,13 @@
         sent = z_buf.at[j, pl.ds(0, p.sources - 2)]
         pltpu.make_async_copy(sent, sent, s2_sem.at[j]).wait()
 
-    @pl.loop(0, p.steps)
+    @pl.loop(0, p.kn)
     def _(c):
-        sent = rot.at[pl.ds(c * p.kc, p.kc), pl.ds(0, (p.devices - 1) * p.share)]
+        sent = rot.at[c, pl.ds(0, (p.devices - 1) * p.share)]
         pltpu.make_async_copy(sent, sent, s1_sem.at[c]).wait()
+
+    @pl.loop(0, p.kb)
+    def _(c):
         sent = rot.at[pl.ds(c, 2), pl.ds(0, (p.ka * p.half - 1) * p.wide)]
         pltpu.make_async_copy(sent, sent, sf_sem.at[c]).wait()
 
@@ -574,58 +659,10 @@
         o_ref[1, :, :, t * p.width : (t + 1) * p.width, :] = x[..., p.bands :]
 
 
-def three_parts(table):
-    high = lax.reduce_precision(table, 8, 7)
-    low = lax.reduce_precision(table - high, 8, 7)
-    return jnp.concatenate([high, low, high], axis=1).astype(jnp.bfloat16)
-
-
-def local_fused(p, bloch, gauge, kq_index, qpoint, re_vectors, re_weight, rp_vectors, rp_weight):
-    real, imag = gauge[0], gauge[1]
-    v_in = jnp.concatenate([jnp.swapaxes(real, 1, 2), jnp.swapaxes(imag, 1, 2)], axis=2)
-    right = jnp.concatenate(
-        [jnp.concatenate([real, imag], axis=2), jnp.concatenate([-imag, real], axis=2)], axis=1
-    )
-    a, b = lax.axis_index("ka"), lax.axis_index("pb")
-    slots = qpoint.reshape(p.pb, p.local_q)
-    other = (b + p.half) % p.pb
-    far_q = lax.dynamic_index_in_dim(slots, other, 0, keepdims=True)
-    far_k = (a * p.local_k + jnp.arange(p.kb, dtype=jnp.int32))[:, None]
-    first = (far_k // (MK2 * MK3) + far_q // (MK2 * MK3)) % MK1
-    second = (far_k // MK3 % MK2 + far_q // MK3 % MK2) % MK2
-    third = (far_k % MK3 + far_q % MK3) % MK3
-    kq_far = (first * MK2 + second) * MK3 + third
-
-    def q_table(vectors, weight, rows):
-        vectors = jnp.repeat(vectors, rows, axis=0)
-        points = jnp.broadcast_to(slots[:, None, :], (p.pb, rows, p.local_q)).reshape(-1)
-        cosine, sine = mesh_phase(vectors, points, p.q_count)
-        row = jnp.arange(vectors.shape[0], dtype=jnp.int32) % rows
-        col = jnp.arange(points.shape[0], dtype=jnp.int32) // p.local_q % rows
-        weight = jnp.repeat(weight, rows).astype(jnp.float32)[:, None]
-        same = row[:, None] == col[None, :]
-        return three_parts(
-            jnp.where(
-                jnp.concatenate([same, same], axis=0),
-                jnp.concatenate([cosine / weight, sine / weight], axis=0),
-                0.0,
-            )
-        )
-
-    tq = q_table(rp_vectors, rp_weight, p.rows)
-    near = p.rp_count // 2
-    start = b // p.half * near
-    tf = q_table(
-        lax.dynamic_slice_in_dim(rp_vectors, start, near),
-        lax.dynamic_slice_in_dim(rp_weight, start, near),
-        2 * p.rows,
-    )
-    points = jnp.arange(p.k_count, dtype=jnp.int32).reshape(p.ka, p.local_k)
-    points = jnp.concatenate([points[:, p.kb :].reshape(-1), points[:, : p.kb].reshape(-1)])
-    cosine, sine = mesh_phase(re_vectors, points, p.k_count)
-    weight = re_weight.astype(jnp.float32)[:, None]
-    tk = three_parts(jnp.concatenate([cosine / weight, sine / weight], axis=0))
-
+def local_fused(p, bloch, gauge, _, qpoint, re_vectors, re_weight, rp_vectors, rp_weight):
+    vectors = jnp.concatenate([re_vectors.T, rp_vectors.T], axis=0)
+    weights = jnp.stack([re_weight, rp_weight])
+    rows_q = 2 * p.rp_count * p.rows
     f32 = jnp.float32
     dma = pltpu.SemaphoreType.DMA
     vmem = pl.BlockSpec(memory_space=pltpu.VMEM)
@@ -634,9 +671,12 @@
     landed = pl.pallas_call(
         functools.partial(kernel, p),
         out_shape=jax.ShapeDtypeStruct((p.rp_local, p.ka, p.block, LANES), f32),
-        in_specs=[any_space, any_space, vmem, smem, smem, vmem, vmem, vmem],
+        in_specs=[any_space, vmem, smem, vmem, vmem, vmem],
         out_specs=any_space,
         scratch_shapes=[
+            pltpu.VMEM((rows_q, 3 * p.rows * p.q_count), jnp.bfloat16),
+            pltpu.VMEM((rows_q, 6 * p.rows * p.q_count), jnp.bfloat16),
+            pltpu.VMEM((2 * p.re_count, 3 * p.k_count), jnp.bfloat16),
             pltpu.VMEM((p.g_slots, 2, p.local_q, p.bands, p.bands), f32),
             pltpu.VMEM((p.k_count, p.bands, LANES), f32),
             pltpu.VMEM((p.local_k, p.devices * p.share, LANES), f32),
@@ -647,15 +687,14 @@
             pltpu.VMEM((p.rp_local, p.sources, p.piece, LANES), f32),
             pltpu.VMEM((p.slots, p.ka, p.block, LANES), f32),
             dma((max(p.g_slots, p.slots),)),
-            dma,
             dma((p.ka,)),
             dma((p.ka,)),
             dma((p.ka,)),
             dma((p.ka,)),
             dma((p.kb,)),
             dma((p.kb,)),
-            dma((p.steps,)),
-            dma((p.steps,)),
+            dma((p.kn,)),
+            dma((p.kn,)),
             dma((p.kb,)),
             dma((p.kb,)),
             dma((p.rp_local,)),
@@ -666,7 +705,7 @@
         compiler_params=pltpu.CompilerParams(
             collective_id=0, has_side_effects=True, vmem_limit_bytes=VMEM_BYTES
         ),
-    )(bloch, v_in, right, kq_index.reshape(-1), kq_far.reshape(-1), tq, tf, tk)
+    )(bloch, gauge, qpoint, qpoint.reshape(1, -1), vectors, weights)
 
     step = p.re_local
     return pl.pallas_call(

time: 534 us -> 505 us (0.946)
  Pallas kernels: 513 us -> 501 us
  other arithmetic: 12 us -> 2.55 us
  local copies, waits for them, and re-layouts: 7.57 us -> 0 us
    pallas_call x1, Pallas kernels: 492 us -> 481 us  [local_fused(): pl.pallas_call(functools.partial(kernel, p), out_shape=jax.ShapeDtypeStru...]
where the time goes in v4:
time: 505 us; the launch traced here: 504 us
  Pallas kernels  501 us (99%)
    pallas_call x1, Pallas kernels, local_fused(): pl.pallas_call(functools.partial(kernel, p), out_shape=jax.ShapeDtypeStru...  481 us
    pallas_call x1, Pallas kernels, local_fused(): pl.pallas_call(functools.partial(unpack, p, step), grid=(p.re_local // st...  20.6 us

profile of v4, /device:TPU:9, one launch (start us, length us, event | category | flops | bytes accessed | tf_op | source)
XLA Modules:
  0.0 503.9 jit_solution(12217665977444615613)
XLA Ops:
  0.0 1.3 pad_add_fusion.1.weights
  1.3 1.3 pad_add_fusion.vectors
  2.6 480.8 %shard_map.73.x_ref = f32[16,4,512,128]{3,2,1,0:T(8,128)} custom-call(f32[2,24,12,64,64]{4,3,2,1,0:T(8,128)} %bloch.1, f32[2,24,64,64]{3,2,1,0:T(8,128)} %gauge.1, s32[96]{0:T(128)} %qpoint.1, s32[1,96]{1,0:T(1,128)} %bitcast.5, s32[6,128]{1,0:T(8,128)} %pad_add_fusion.vectors, s32[2,128]{1,0:T(2,128)} %pad_add_fusion.1.weights), custom_call_target="tpu_custom_call" | custom-call | tf_op jit(solution)/shard_map/pallas_call | solution.py:671
  483.3 20.6 %shard_map.74 = f32[2,32,16,64,64]{4,3,2,1,0:T(8,128)} custom-call(f32[16,4,512,128]{3,2,1,0:T(8,128)} %shard_map.73.x_ref), custom_call_target="tpu_custom_call" | custom-call | tf_op jit(solution)/shard_map/pallas_call | solution.py:711

commit v5 on v4

--- a/solution.py
+++ b/solution.py
@@ -12,6 +12,7 @@
 MK2 = 6
 MK3 = 4
 LANES = 128
+UNPACK_SLOTS = 8
 VMEM_BYTES = 67_000_000
 MESH = pl.DeviceIdType.MESH
 
@@ -133,21 +134,23 @@
         self.share = self.rows * local_q
         self.wide = 2 * self.share
         self.width = self.rows * pb
-        self.piece = self.rows * ka * self.kn
+        self.piece = ka * self.kn
+        self.chunks = self.rp_local * self.rows
         self.sources = pb + self.half
-        self.block = self.re_local * self.width
+        self.block = self.re_local * pb
         self.raw_ahead = min(3, self.kb)
         self.g_slots = 3
         self.slots = 2
-        self.ahead = 2
+        self.ahead = 4
         self.fits = (
             self.share % 8 == 0
             and self.k_count % 16 == 0
             and self.kb % 2 == 0
             and (ka * self.kb) % 8 == 0
             and (pb * self.share) % 16 == 0
-            and self.width % 8 == 0
-            and self.rp_local > self.slots
+            and pb % 8 == 0
+            and self.chunks > self.slots
+            and self.rp_local > UNPACK_SLOTS
         )
 
 
@@ -188,14 +191,14 @@
     table[...] = full.astype(jnp.bfloat16)
 
 
-def make_tables(p, side, slots, vectors, weights, tq, tf, tk):
+def make_tables(p, side, slots, re, rp, tq, tf, tk):
     f32 = jnp.float32
     iota = lambda shape, dim: lax.broadcasted_iota(jnp.int32, shape, dim)
-    rp = jnp.concatenate([vectors[3:6], weights[1:2]], axis=0).astype(f32)
-    re = jnp.concatenate([vectors[0:3], weights[0:1]], axis=0).astype(f32)
-
-    def q_table(table, start, count, rows):
+    re, rp = re.astype(f32), rp.astype(f32)
+
+    def q_table(table, start, count, rows, inner):
         row = iota((count * rows, 1), 0)
+        band = row % rows % inner * (rows // inner) + row % rows // inner
         columns = pick(start + row // rows, rp)
         width = rows * p.q_count
         col = iota((1, width), 1)
@@ -204,11 +207,11 @@
         held = jnp.broadcast_to(slots[...], (8, p.q_count)).astype(f32)
         points = dot(held.astype(jnp.bfloat16), chosen.astype(jnp.bfloat16))[0:1]
         cosine, sine = phases(columns, points.astype(jnp.int32), p.q_count)
-        same = row % rows == col // p.local_q % rows
+        same = band == col // p.local_q % rows
         put_table(table, jnp.where(same, cosine, 0.0), jnp.where(same, sine, 0.0))
 
-    q_table(tq, 0, p.rp_count, p.rows)
-    q_table(tf, side * (p.rp_count // 2), p.rp_count // 2, 2 * p.rows)
+    q_table(tq, 0, p.rp_count, p.rows, 1)
+    q_table(tf, side * (p.rp_count // 2), p.rp_count // 2, 2 * p.rows, 2)
 
     columns = pick(iota((p.re_count, 1), 0), re)
     col = iota((1, p.k_count), 1)
@@ -228,8 +231,10 @@
     gauge,
     qpoint,
     slots,
-    vectors,
-    weights,
+    re_vectors,
+    re_weight,
+    rp_vectors,
+    rp_weight,
     out,
     tq,
     tf,
@@ -294,9 +299,12 @@
 
     @pl.loop(0, p.local_k)
     def _(k):
-        vg[a * p.local_k + k] = jnp.concatenate(
-            [jnp.transpose(gauge[0, k]), jnp.transpose(gauge[1, k])], axis=1
-        )
+        v = jnp.concatenate([jnp.transpose(gauge[0, k]), jnp.transpose(gauge[1, k])], axis=1)
+        for t in range(p.ka):
+            for r in range(p.rows):
+                first = t * p.width + r * p.pb
+                where = pl.ds(t * p.width + r, p.pb, stride=p.rows)
+                vg[a * p.local_k + k, where, :] = v[first : first + p.pb]
 
     pl.semaphore_wait(barrier, p.devices - 1)
 
@@ -365,7 +373,9 @@
         send_0(k).start()
 
     lax.fori_loop(p.raw_ahead, middle, right_side, 0)
-    make_tables(p, side, slots, vectors, weights, tq, tf, tk)
+    re = jnp.concatenate([re_vectors[...], re_weight[...]], axis=0)
+    rp = jnp.concatenate([rp_vectors[...], rp_weight[...]], axis=0)
+    make_tables(p, side, slots, re, rp, tq, tf, tk)
     for i in range(1, p.ka):
         send_v(i).wait_recv()
         pass_v(i).start()
@@ -431,7 +441,7 @@
             where = pl.ds(first + j * gap, rows, stride=stride)
             y_buf[where, :] = y[:rows, cols] + swap(y[rows:, cols], sign)
 
-    far_first = p.pb * p.rp_local * p.piece
+    far_first = p.pb * p.chunks * p.piece
 
     def sum_near(c):
         part = x_buf.at[:, pl.ds(c, 1)]
@@ -516,7 +526,7 @@
     def send_2(j, o):
         t = xor(b, o, p.pb)
         return pltpu.make_async_remote_copy(
-            src_ref=y_buf.at[pl.ds((t * p.rp_local + j) * p.piece, p.piece)],
+            src_ref=y_buf.at[pl.ds((t * p.chunks + j) * p.piece, p.piece)],
             dst_ref=z_buf.at[j, b],
             send_sem=s2_sem.at[j],
             recv_sem=r2_sem.at[j],
@@ -527,7 +537,7 @@
     def send_2f(j, o):
         t = xor(seat, o, p.half)
         return pltpu.make_async_remote_copy(
-            src_ref=y_buf.at[pl.ds(((p.pb + t) * p.rp_local + j) * p.piece, p.piece)],
+            src_ref=y_buf.at[pl.ds(((p.pb + t) * p.chunks + j) * p.piece, p.piece)],
             dst_ref=z_buf.at[j, p.pb + seat],
             send_sem=s2_sem.at[j],
             recv_sem=r2_sem.at[j],
@@ -546,7 +556,7 @@
 
         for mine in (b, p.pb + seat):
             pltpu.make_async_copy(
-                y_buf.at[pl.ds((mine * p.rp_local + j) * p.piece, p.piece)],
+                y_buf.at[pl.ds((mine * p.chunks + j) * p.piece, p.piece)],
                 z_buf.at[j, mine],
                 r2_sem.at[j],
             ).start()
@@ -576,14 +586,14 @@
         pltpu.make_async_copy(sent, sent, s3_sem.at[slot]).wait()
         own_3(j).wait()
 
-    near, less = p.ka * p.kn, p.ka * p.kb
-
-    @pl.loop(0, p.rp_local)
+    less = p.ka * p.kb
+
+    @pl.loop(0, p.chunks)
     def _(j):
         pltpu.make_async_copy(z_buf.at[j], z_buf.at[j], r2_sem.at[j]).wait()
         slot = j % p.slots
 
-        @pl.when(j + p.ahead < p.rp_local)
+        @pl.when(j + p.ahead < p.chunks)
         def _():
             start_2(j + p.ahead)
 
@@ -591,35 +601,26 @@
         def _():
             free_3(j - p.slots)
 
-        @pl.loop(0, p.pb)
-        def _(source):
-            for r in range(0, p.rows, 2):
-                z = jnp.concatenate(
-                    [
-                        jnp.concatenate(
-                            [
-                                z_buf[j, source, (r + s) * near : (r + s + 1) * near, :],
-                                z_buf[
-                                    j,
-                                    p.pb + source // 2,
-                                    pl.ds((source % 2 * p.rows + r + s) * less, less),
-                                    :,
-                                ],
-                            ],
-                            axis=0,
-                        )
-                        for s in range(2)
-                    ],
-                    axis=1,
-                )
-                z_high, z_low = split(z)
-                w = dot(tk[...], jnp.concatenate([z_high, z_high, z_low], axis=0))
-                for s in range(2):
-                    cols = slice(s * LANES, (s + 1) * LANES)
-                    full = w[: p.re_count, cols] + swap(w[p.re_count :, cols], sign)
-                    where = pl.ds(source * p.rows + r + s, p.re_local, stride=p.width)
-                    for t in range(p.ka):
-                        w_buf[slot, t, where, :] = full[t * p.re_local : (t + 1) * p.re_local]
+        @pl.loop(0, p.half)
+        def _(s):
+            far_part = z_buf[j, p.pb + s]
+            z = jnp.concatenate(
+                [
+                    jnp.concatenate(
+                        [z_buf[j, 2 * s + i], far_part[i * less : (i + 1) * less]], axis=0
+                    )
+                    for i in range(2)
+                ],
+                axis=1,
+            )
+            z_high, z_low = split(z)
+            w = dot(tk[...], jnp.concatenate([z_high, z_high, z_low], axis=0))
+            for i in range(2):
+                cols = slice(i * LANES, (i + 1) * LANES)
+                full = w[: p.re_count, cols] + swap(w[p.re_count :, cols], sign)
+                where = pl.ds(2 * s + i, p.re_local, stride=p.pb)
+                for t in range(p.ka):
+                    w_buf[slot, t, where, :] = full[t * p.re_local : (t + 1) * p.re_local]
 
         @pl.loop(1, p.ka)
         def _(o):
@@ -627,10 +628,10 @@
 
         own_3(j).start()
 
-    for j in range(p.rp_local - p.slots, p.rp_local):
+    for j in range(p.chunks - p.slots, p.chunks):
         free_3(j)
 
-    @pl.loop(0, p.rp_local)
+    @pl.loop(0, p.chunks)
     def _(j):
         into = out.at[j, pl.ds(0, p.ka - 1)]
         pltpu.make_async_copy(into, into, r3_sem.at[j]).wait()
@@ -652,16 +653,46 @@
         pass_v(i).wait_send()
 
 
-def unpack(p, step, x_ref, o_ref):
-    for t in range(p.ka):
-        x = x_ref[0, t].reshape(step, 1, p.width, LANES)
-        o_ref[0, :, :, t * p.width : (t + 1) * p.width, :] = x[..., : p.bands]
-        o_ref[1, :, :, t * p.width : (t + 1) * p.width, :] = x[..., p.bands :]
+def unpack(p, x_ref, o_ref, x_buf, o_buf, x_sem, o_sem):
+    def load(j):
+        slot = j % UNPACK_SLOTS
+        return pltpu.make_async_copy(
+            x_ref.at[pl.ds(j * p.rows, p.rows)], x_buf.at[slot], x_sem.at[slot]
+        )
+
+    def store(j):
+        slot = j % UNPACK_SLOTS
+        return pltpu.make_async_copy(o_buf.at[slot], o_ref.at[:, :, j], o_sem.at[slot])
+
+    for j in range(UNPACK_SLOTS):
+        load(j).start()
+
+    @pl.loop(0, p.rp_local)
+    def _(j):
+        slot = j % UNPACK_SLOTS
+        load(j).wait()
+
+        @pl.when(j >= UNPACK_SLOTS)
+        def _():
+            store(j - UNPACK_SLOTS).wait()
+
+        for r in range(p.rows):
+            for t in range(p.ka):
+                x = x_buf[slot, r, t].reshape(p.re_local, p.pb, LANES)
+                first = t * p.width + r * p.pb
+                o_buf[slot, 0, :, first : first + p.pb, :] = x[..., : p.bands]
+                o_buf[slot, 1, :, first : first + p.pb, :] = x[..., p.bands :]
+        store(j).start()
+
+        @pl.when(j + UNPACK_SLOTS < p.rp_local)
+        def _():
+            load(j + UNPACK_SLOTS).start()
+
+    for j in range(p.rp_local - UNPACK_SLOTS, p.rp_local):
+        store(j).wait()
 
 
 def local_fused(p, bloch, gauge, _, qpoint, re_vectors, re_weight, rp_vectors, rp_weight):
-    vectors = jnp.concatenate([re_vectors.T, rp_vectors.T], axis=0)
-    weights = jnp.stack([re_weight, rp_weight])
     rows_q = 2 * p.rp_count * p.rows
     f32 = jnp.float32
     dma = pltpu.SemaphoreType.DMA
@@ -670,8 +701,8 @@
     smem = pl.BlockSpec(memory_space=pltpu.SMEM)
     landed = pl.pallas_call(
         functools.partial(kernel, p),
-        out_shape=jax.ShapeDtypeStruct((p.rp_local, p.ka, p.block, LANES), f32),
-        in_specs=[any_space, vmem, smem, vmem, vmem, vmem],
+        out_shape=jax.ShapeDtypeStruct((p.chunks, p.ka, p.block, LANES), f32),
+        in_specs=[any_space, vmem, smem, vmem, vmem, vmem, vmem, vmem],
         out_specs=any_space,
         scratch_shapes=[
             pltpu.VMEM((rows_q, 3 * p.rows * p.q_count), jnp.bfloat16),
@@ -683,8 +714,8 @@
             pltpu.VMEM((p.kb, p.devices * p.share, LANES), f32),
             pltpu.VMEM((p.ka, p.kn, p.pb, p.share, LANES), f32),
             pltpu.VMEM((p.ka, p.kb, p.pb, p.wide, LANES), f32),
-            pltpu.VMEM((p.sources * p.rp_local * p.piece, LANES), f32),
-            pltpu.VMEM((p.rp_local, p.sources, p.piece, LANES), f32),
+            pltpu.VMEM((p.sources * p.chunks * p.piece, LANES), f32),
+            pltpu.VMEM((p.chunks, p.sources, p.piece, LANES), f32),
             pltpu.VMEM((p.slots, p.ka, p.block, LANES), f32),
             dma((max(p.g_slots, p.slots),)),
             dma((p.ka,)),
@@ -697,29 +728,37 @@
             dma((p.kn,)),
             dma((p.kb,)),
             dma((p.kb,)),
-            dma((p.rp_local,)),
-            dma((p.rp_local,)),
+            dma((p.chunks,)),
+            dma((p.chunks,)),
             dma((p.slots,)),
-            dma((p.rp_local,)),
+            dma((p.chunks,)),
         ],
         compiler_params=pltpu.CompilerParams(
             collective_id=0, has_side_effects=True, vmem_limit_bytes=VMEM_BYTES
         ),
-    )(bloch, gauge, qpoint, qpoint.reshape(1, -1), vectors, weights)
-
-    step = p.re_local
+    )(
+        bloch,
+        gauge,
+        qpoint,
+        qpoint.reshape(1, -1),
+        re_vectors.T,
+        re_weight.reshape(1, -1),
+        rp_vectors.T,
+        rp_weight.reshape(1, -1),
+    )
+
     return pl.pallas_call(
-        functools.partial(unpack, p, step),
-        grid=(p.re_local // step, p.rp_local),
+        functools.partial(unpack, p),
         out_shape=jax.ShapeDtypeStruct((2, p.re_local, p.rp_local, p.bands, p.bands), f32),
-        in_specs=[
-            pl.BlockSpec(
-                (1, p.ka, step * p.width, LANES), lambda i, j: (j, 0, i, 0)
-            )
+        in_specs=[any_space],
+        out_specs=any_space,
+        scratch_shapes=[
+            pltpu.VMEM((UNPACK_SLOTS, p.rows, p.ka, p.block, LANES), f32),
+            pltpu.VMEM((UNPACK_SLOTS, 2, p.re_local, p.bands, p.bands), f32),
+            dma((UNPACK_SLOTS,)),
+            dma((UNPACK_SLOTS,)),
         ],
-        out_specs=pl.BlockSpec(
-            (2, step, 1, p.bands, p.bands), lambda i, j: (0, i, j, 0, 0)
-        ),
+        compiler_params=pltpu.CompilerParams(vmem_limit_bytes=VMEM_BYTES),
     )(landed)
 
 

time: 505 us -> 493 us (0.976)
  Pallas kernels: 501 us -> 492 us
where the time goes in v5:
time: 493 us; the launch traced here: 492 us
  Pallas kernels  492 us (100%)
    pallas_call x1, Pallas kernels, local_fused(): pl.pallas_call(functools.partial(kernel, p), out_shape=jax.ShapeDtypeStru...  476 us
    pallas_call x1, Pallas kernels, local_fused(): pl.pallas_call(functools.partial(unpack, p), out_shape=jax.ShapeDtypeStru...  15.9 us

profile of v5, /device:TPU:9, one launch (start us, length us, event | category | flops | bytes accessed | tf_op | source)
XLA Modules:
  0.0 491.7 jit_solution(3279164094607157947)
XLA Ops:
  0.0 475.8 %shard_map.73.x_ref = f32[32,4,256,128]{3,2,1,0:T(8,128)} custom-call(f32[2,24,12,64,64]{4,3,2,1,0:T(8,128)} %bloch.1, f32[2,24,64,64]{3,2,1,0:T(8,128)} %gauge.1, s32[96]{0:T(128)} %qpoint.1, s32[1,96]{1,0:T(1,128)} %bitcast.7, s32[3,128]{1,0:T(4,128)} %bitcast.5, s32[1,128]{1,0:T(1,128)} %bitcast.8, s32[3,128]{1,0:T(4,128)} %bitcast.6, s32[1,128]{1,0:T(1,128)} %bitcast.9), custom_call_target="tpu_custom_call" | custom-call | tf_op jit(solution)/shard_map/pallas_call | solution.py:702
  475.8 15.9 %shard_map.74 = f32[2,32,16,64,64]{4,3,2,1,0:T(8,128)} custom-call(f32[32,4,256,128]{3,2,1,0:T(8,128)} %shard_map.73.x_ref), custom_call_target="tpu_custom_call" | custom-call | tf_op jit(solution)/shard_map/pallas_call | solution.py:750

commit v6 on v5

--- a/solution.py
+++ b/solution.py
@@ -228,7 +228,7 @@
 def kernel(
     p,
     bloch,
-    gauge,
+    gauge_in,
     qpoint,
     slots,
     re_vectors,
@@ -239,6 +239,7 @@
     tq,
     tf,
     tk,
+    gauge,
     gbuf,
     vg,
     rot,
@@ -249,6 +250,7 @@
     z_buf,
     w_buf,
     g_sem,
+    u_sem,
     vs_sem,
     v1_sem,
     f_sem,
@@ -286,6 +288,8 @@
         slot = k % p.g_slots
         return pltpu.make_async_copy(bloch.at[:, k], gbuf.at[slot], g_sem.at[slot])
 
+    load_u = pltpu.make_async_copy(gauge_in, gauge, u_sem)
+    load_u.start()
     for k in range(p.g_slots):
         load_g(k).start()
 
@@ -296,6 +300,8 @@
     def _(o):
         t = (me + o) % p.devices
         pl.semaphore_signal(barrier, inc=1, device_id=(t // p.pb, t % p.pb), device_id_type=MESH)
+
+    load_u.wait()
 
     @pl.loop(0, p.local_k)
     def _(k):
@@ -483,45 +489,57 @@
     def begin(c):
         return c * c * p.kn // (p.kb * p.kb)
 
-    @pl.loop(0, p.kb + 1)
+    def stay(c):
+        @pl.loop(begin(c), begin(c + 1))
+        def _(k):
+            left_side(rot, p.kb + k, p.kb + k, b)
+
+            @pl.loop(0, p.devices - 1)
+            def _(n):
+                send_1(k, n).start()
+
+            own_1(k).start()
+
+    def swapped(c):
+        send_0(c).wait_send()
+        left_side(rot, c, c, b)
+
+        @pl.loop(0, p.ka * p.half - 1)
+        def _(n):
+            send_f(rot, c, b, n).start()
+
+        own_f(rot, c, b).start()
+        send_0(c).wait_recv()
+        left_side(far, c, c, other)
+
+        @pl.loop(0, p.ka * p.half - 1)
+        def _(n):
+            send_f(far, c, other, n).start()
+
+        own_f(far, c, other).start()
+
+    @pl.loop(0, p.kb + 2)
     def _(c):
         @pl.when(c < p.kb)
         def _():
-            send_0(c).wait_send()
-            left_side(rot, c, c, b)
-
-            @pl.loop(0, p.ka * p.half - 1)
-            def _(n):
-                send_f(rot, c, b, n).start()
-
-            own_f(rot, c, b).start()
-            send_0(c).wait_recv()
-            left_side(far, c, c, other)
-
-            @pl.loop(0, p.ka * p.half - 1)
-            def _(n):
-                send_f(far, c, other, n).start()
-
-            own_f(far, c, other).start()
-
-            @pl.loop(begin(c), begin(c + 1))
-            def _(k):
-                left_side(rot, p.kb + k, p.kb + k, b)
-
-                @pl.loop(0, p.devices - 1)
-                def _(n):
-                    send_1(k, n).start()
-
-                own_1(k).start()
+            @pl.loop(0, 2)
+            def _(turn):
+                @pl.when(turn == core)
+                def _():
+                    swapped(c)
+
+                @pl.when(turn != core)
+                def _():
+                    stay(c)
 
             @pl.when(c + p.raw_ahead < p.kb)
             def _():
                 send_0(c + p.raw_ahead).start()
 
-        @pl.when(c > 0)
+        @pl.when(c >= 2)
         def _():
-            sum_far(c - 1)
-            pl.loop(begin(c - 1), begin(c))(sum_near)
+            sum_far(c - 2)
+            pl.loop(begin(c - 2), begin(c - 2 + 1))(sum_near)
 
     def send_2(j, o):
         t = xor(b, o, p.pb)
@@ -702,12 +720,13 @@
     landed = pl.pallas_call(
         functools.partial(kernel, p),
         out_shape=jax.ShapeDtypeStruct((p.chunks, p.ka, p.block, LANES), f32),
-        in_specs=[any_space, vmem, smem, vmem, vmem, vmem, vmem, vmem],
+        in_specs=[any_space, any_space, smem, vmem, vmem, vmem, vmem, vmem],
         out_specs=any_space,
         scratch_shapes=[
             pltpu.VMEM((rows_q, 3 * p.rows * p.q_count), jnp.bfloat16),
             pltpu.VMEM((rows_q, 6 * p.rows * p.q_count), jnp.bfloat16),
             pltpu.VMEM((2 * p.re_count, 3 * p.k_count), jnp.bfloat16),
+            pltpu.VMEM((2, p.local_k, p.bands, p.bands), f32),
             pltpu.VMEM((p.g_slots, 2, p.local_q, p.bands, p.bands), f32),
             pltpu.VMEM((p.k_count, p.bands, LANES), f32),
             pltpu.VMEM((p.local_k, p.devices * p.share, LANES), f32),
@@ -718,6 +737,7 @@
             pltpu.VMEM((p.chunks, p.sources, p.piece, LANES), f32),
             pltpu.VMEM((p.slots, p.ka, p.block, LANES), f32),
             dma((max(p.g_slots, p.slots),)),
+            dma,
             dma((p.ka,)),
             dma((p.ka,)),
             dma((p.ka,)),

time: 493 us -> 493 us (level)
  no operation moved by 1% of the time
where the time goes in v6:
time: 493 us; the launch traced here: 492 us
  Pallas kernels  492 us (100%)
    pallas_call x1, Pallas kernels, local_fused(): pl.pallas_call(functools.partial(kernel, p), out_shape=jax.ShapeDtypeStru...  476 us
    pallas_call x1, Pallas kernels, local_fused(): pl.pallas_call(functools.partial(unpack, p), out_shape=jax.ShapeDtypeStru...  15.9 us

profile of v6, /device:TPU:9, one launch (start us, length us, event | category | flops | bytes accessed | tf_op | source)
XLA Modules:
  0.0 492.3 jit_solution(1321890291567494293)
XLA Ops:
  0.0 476.3 %shard_map.73.x_ref = f32[32,4,256,128]{3,2,1,0:T(8,128)} custom-call(f32[2,24,12,64,64]{4,3,2,1,0:T(8,128)} %bloch.1, f32[2,24,64,64]{3,2,1,0:T(8,128)} %gauge_in.1, s32[96]{0:T(128)} %qpoint.1, s32[1,96]{1,0:T(1,128)} %bitcast.7, s32[3,128]{1,0:T(4,128)} %bitcast.5, s32[1,128]{1,0:T(1,128)} %bitcast.8, s32[3,128]{1,0:T(4,128)} %bitcast.6, s32[1,128]{1,0:T(1,128)} %bitcast.9), custom_call_target="tpu_custom_call" | custom-call | tf_op jit(solution)/shard_map/pallas_call | solution.py:720
  476.3 15.9 %shard_map.74 = f32[2,32,16,64,64]{4,3,2,1,0:T(8,128)} custom-call(f32[32,4,256,128]{3,2,1,0:T(8,128)} %shard_map.73.x_ref), custom_call_target="tpu_custom_call" | custom-call | tf_op jit(solution)/shard_map/pallas_call | solution.py:770
